TPU v7x, 128 devices: a whole 4x4x4 slice. The times are simulated.
128 devices in a mesh: gx: 4 (over z), gy: 4 (over y), gz: 8 (over x, core).
Axes of the slice: x: 4, y: 4, z: 4, core: 2. Of those that a mesh axis runs over, the one named last changes fastest.
Arguments:
- interact: bfloat16 [16, 32768, 512], P(None, ('gx', 'gy', 'gz')), may hold values from -6 to 6
- weight_one: bfloat16 [512, 1024], replicated, may hold values from -0.25 to 0.25
- bias_one: float32 [1024], replicated, may hold values from -3 to 3
- weight_two: bfloat16 [1024, 1024], replicated, may hold values from -0.1875 to 0.1875
- bias_two: float32 [1024], replicated, may hold values from -3 to 3
- weight_three: bfloat16 [1024, 512], replicated, may hold values from -0.1875 to 0.1875
- bias_three: float32 [512], replicated, may hold values from -3 to 3
- weight_four: bfloat16 [512, 256], replicated, may hold values from -0.25 to 0.25
- bias_four: float32 [256], replicated, may hold values from -3 to 3
- weight_out: bfloat16 [256, 1], replicated, may hold values from -1 to 1
- bias_out: float32 [1], replicated, may hold values from -1.5 to 0
- bucket_index: int32 [16, 32768], P(None, ('gx', 'gy', 'gz')), may hold values from 0 to 4095
- labels: int32 [16, 32768], P(None, ('gx', 'gy', 'gz')), may hold values from 0 to 1
Outputs:
- bucket_stats: float32 [16, 4, 4096], P(None, None, 'gx')
- summary: float32 [16, 4], replicated
All inputs are finite; a program needn't handle non-finite values.
Results may differ from a plain program's by a relative error of at most 0.0045.
Values sent between devices are 32-bit elements; how exact they have to be, the bound alone decides.
No kernel may reach another device: no remote copies, remote signals or barrier semaphores. Data moves between devices by JAX's collectives and lax.ppermute only.
A program may use at most 128 MiB of HBM per device.

v0:
```python
import jax
import jax.numpy as jnp
from jax import lax
from jax.sharding import PartitionSpec as P

NBUCK = 4096


def split_up(value, dim, size):
    before, after = (value.shape[:dim], value.shape[dim + 1 :])
    return jnp.moveaxis(value.reshape(*before, size, -1, *after), dim, 0)


def sent_and_summed(value, axis, dim):
    tiles = split_up(value, dim, lax.axis_size(axis))
    arrived = lax.all_to_all(tiles, axis, split_axis=0, concat_axis=0, tiled=True)
    return arrived.sum(axis=0)


def gathered_total(value, axis):
    tiles = lax.all_gather(value, axis)
    return tiles.sum(axis=0)


def from_everyone(value, axis):
    size = lax.axis_size(axis)
    return lax.all_to_all(
        jnp.broadcast_to(value[None], (size, *value.shape)), axis, 0, 0, tiled=True
    )


def folded_in_pairs(pieces, combine):
    while len(jax.tree.leaves(pieces)[0]) > 1:
        pieces = jax.vmap(combine)(*(pieces[side::2] for side in (0, 1)))
    return pieces[0]


def carried_in(value, axis, combine, identity):
    size, index = (lax.axis_size(axis), lax.axis_index(axis))
    passed = jnp.arange(size) < index

    def kept(part, zero, own):
        part = jnp.where(
            passed.reshape(-1, *(1 for _ in own.shape)), part, jnp.asarray(zero, own.dtype)
        )
        return part

    pieces = from_everyone(value, axis)
    return folded_in_pairs(kept(pieces, identity, value), combine)


def one_axis_at_a_time(value, axes):
    for axis in axes:
        value = lax.psum(value, axis)
    return value


def joined_along(tiles, dim):
    shape = list(tiles.shape[1:])
    shape[dim] *= tiles.shape[0]
    return jnp.moveaxis(tiles, 0, dim).reshape(shape)


def gather_directly(value, axis, dim):
    tiles = from_everyone(value, axis)
    return joined_along(tiles, dim)


def layer_relu(inputs, weight, offset):
    return jax.nn.relu(jnp.dot(inputs, weight, preferred_element_type=jnp.float32) + offset).astype(
        jnp.bfloat16
    )


def bucket_reports(totals):
    positives = totals[:, 0]
    negatives = totals[:, 1]
    counts = jnp.maximum(positives + negatives, 1.0)
    return jnp.stack(
        [positives / counts, totals[:, 2] / counts, totals[:, 3] / counts, totals[:, 4] / counts],
        axis=1,
    )


def summarize(numerator, column_sums):
    pair_count = jnp.maximum(column_sums[:, 0] * column_sums[:, 1], 1.0)
    example_count = jnp.maximum(column_sums[:, 0] + column_sums[:, 1], 1.0)
    return jnp.stack(
        [
            numerator / pair_count,
            column_sums[:, 3] / example_count,
            column_sums[:, 2] / jnp.maximum(column_sums[:, 0], 1.0),
            column_sums[:, 4] / example_count,
        ],
        axis=1,
    )


def combine_add(earlier, later):
    return earlier + later


def split_parts(values):
    upper = values.astype(jnp.bfloat16)
    remain = values - upper.astype(jnp.float32)
    middle = remain.astype(jnp.bfloat16)
    lower = (remain - middle.astype(jnp.float32)).astype(jnp.bfloat16)
    return jnp.concatenate([upper, middle, lower], axis=0)


def merge_reports(histograms):
    bucket_share = sent_and_summed(histograms, ("gx", "gy"), 2)
    bucket_share = gathered_total(bucket_share, "gz")
    reports = bucket_reports(bucket_share)
    negatives = bucket_share[:, 1]
    negative_sums = jnp.sum(negatives, axis=1)
    before = carried_in(negative_sums, ("gx", "gy"), combine_add, jnp.zeros_like(negative_sums))
    below_count = before[:, None] + jnp.cumsum(negatives, axis=1) - negatives
    partial_numerator = jnp.sum(bucket_share[:, 0] * (below_count + 0.5 * negatives), axis=1)
    numerator, column_sums = (
        one_axis_at_a_time(partial_numerator, ("gx", "gy")),
        one_axis_at_a_time(jnp.sum(bucket_share, axis=2), ("gx", "gy")),
    )
    report_block = gather_directly(reports, "gy", 2)
    return (report_block, summarize(numerator, column_sums))


def on_device(
    interact,
    weight_one,
    bias_one,
    weight_two,
    bias_two,
    weight_three,
    bias_three,
    weight_four,
    bias_four,
    weight_out,
    bias_out,
    bucket_index,
    labels,
):
    intervals, local_rows, features_in = interact.shape
    flat_rows = interact.reshape(intervals * local_rows, features_in)
    hidden = layer_relu(flat_rows, weight_one, bias_one)
    hidden = layer_relu(hidden, weight_two, bias_two)
    hidden = layer_relu(hidden, weight_three, bias_three)
    hidden = layer_relu(hidden, weight_four, bias_four)
    logits = jnp.dot(hidden, weight_out, preferred_element_type=jnp.float32)[:, 0] + bias_out[0]
    logits = logits.reshape(intervals, local_rows)
    observed = labels.astype(jnp.float32)
    predicted = jax.nn.sigmoid(logits)
    losses = jax.nn.softplus(logits) - observed * logits
    squared = (predicted - observed) ** 2
    values = jnp.stack([observed, 1.0 - observed, predicted, losses, squared], axis=1)
    bucket_ids = lax.broadcasted_iota(jnp.int32, (1, NBUCK), 1)

    def histogram_one(inputs):
        row_values, buckets = inputs
        one_hot = (buckets[:, None] == bucket_ids).astype(jnp.bfloat16)
        parts = split_parts(row_values)
        partial_value = jnp.dot(parts, one_hot, preferred_element_type=jnp.float32)
        return jnp.sum(partial_value.reshape(3, row_values.shape[0], NBUCK), axis=0)

    histograms = lax.map(histogram_one, (values, bucket_index))
    bucket_stats, summary = merge_reports(histograms)
    return (bucket_stats, summary)


def solution(mesh):
    in_specs = (
        P(None, ("gx", "gy", "gz"), None),
        P(),
        P(),
        P(),
        P(),
        P(),
        P(),
        P(),
        P(),
        P(),
        P(),
        P(None, ("gx", "gy", "gz")),
        P(None, ("gx", "gy", "gz")),
    )
    out_specs = (P(None, None, "gx"), P())
    return jax.shard_map(
        on_device, mesh=mesh, in_specs=in_specs, out_specs=out_specs, check_vma=False
    )
```

profile of v0, /device:TPU:0, one launch (start us, length us, event | category | flops | bytes accessed | tf_op | source)
XLA Modules:
  0.0 154.5 jit_solution(18154456367741899383)
XLA Ops:
  1.4 0.8 copy-done
  2.3 18.6 %fusion.11 = f32[4096,1024]{1,0:T(8,128)} fusion(bf16[1024,1024]{1,0:T(8,128)(2,1)S(1)} %copy-done, f32[1024]{0:T(1024)} %param.17, bf16[4096,512]{1,0:T(8,128)(2,1)} %bitcast.83, bf16[512,1024]{1,0:T(8,128)(2,1)} %param.16), kind=kOutput, calls=%fused_computation.18 | convolution fusion | flops 12897484800 | bytes 24121344 | tf_op jit(solution)/shard_map/dot_general | solution.py:70
  20.9 10.5 %fusion.20 = bf16[4096,256]{1,0:T(8,128)(2,1)} fusion(bf16[512,256]{1,0:T(8,128)(2,1)S(1)} %copy-done.4, bf16[1024,512]{1,0:T(8,128)(2,1)S(1)} %copy-done.3, f32[4096,1024]{1,0:T(8,128)} %fusion.11, f32[1024]{0:T(1024)S(1)} %copy-done.5, f32[512]{0:T(512)S(1)} %copy-done.6, f32[256]{0:T(256)S(1)} %copy-done.7), kind=kOutput, calls=%fused_computation.28 | convolution fusion | flops 5390729216 | bytes 20192256 | tf_op jit(solution)/shard_map/dot_general | solution.py:70
  31.4 2.2 %fusion.34 = f32[1,4096]{1,0:T(1,128)S(1)} fusion(bf16[4096,256]{1,0:T(8,128)(2,1)} %fusion.20, bf16[256,1]{0,1:T(2,128)(2,1)S(1)} %copy-done.2), kind=kOutput, calls=%fused_computation.66 | convolution fusion | flops 2097152 | bytes 2114048 | tf_op jit(solution)/shard_map/dot_general | solution.py:149
  34.0 36.2 %while.11 = (s32[]{:T(128)}, f32[16,5,4096]{2,1,0:T(8,128)}, f32[16,5,256]{2,1,0:T(8,128)S(1)}, s32[16,256]{1,0:T(8,128)}, s32[]{:T(128)}, /*index=5*/f32[]{:T(128)}) while((s32[]{:T(128)}, f32[16,5,4096]{2,1,0:T(8,128)}, f32[16,5,256]{2,1,0:T(8,128)S(1)}, s32[16,256]{1,0:T(8,128)}, s32[]{:T(128)}, /*index=5*/f32[]{:T(128)}) %tuple.41), condition=%wide.region_2.3_spmd.clone, body=%wide.region_0.2_spmd.clone.sunk | while | flops 32577536 | bytes 1304657 | solution.py:165
  34.0 0.7 constant_dynamic-slice_fusion.2
  34.7 0.8 fusion.45
  36.3 0.7 constant_dynamic-slice_fusion.2
  37.0 0.8 fusion.45
  37.8 0.7 bitcast_dynamic-update-slice_fusion.2
  38.5 0.7 constant_dynamic-slice_fusion.2
  39.2 0.8 fusion.45
  40.1 0.7 bitcast_dynamic-update-slice_fusion.2
  40.8 0.7 constant_dynamic-slice_fusion.2
  41.5 0.8 fusion.45
  42.4 0.7 bitcast_dynamic-update-slice_fusion.2
  43.1 0.7 constant_dynamic-slice_fusion.2
  43.8 0.8 fusion.45
  44.6 0.7 bitcast_dynamic-update-slice_fusion.2
  45.3 0.7 constant_dynamic-slice_fusion.2
  46.0 0.8 fusion.45
  46.9 0.7 bitcast_dynamic-update-slice_fusion.2
  47.6 0.7 constant_dynamic-slice_fusion.2
  48.3 0.8 fusion.45
  49.2 0.7 bitcast_dynamic-update-slice_fusion.2
  49.8 0.7 constant_dynamic-slice_fusion.2
  50.5 0.8 fusion.45
  51.4 0.7 bitcast_dynamic-update-slice_fusion.2
  52.1 0.7 constant_dynamic-slice_fusion.2
  52.8 0.8 fusion.45
  53.7 0.7 bitcast_dynamic-update-slice_fusion.2
  54.4 0.7 constant_dynamic-slice_fusion.2
  55.1 0.8 fusion.45
  55.9 0.7 bitcast_dynamic-update-slice_fusion.2
  56.6 0.7 constant_dynamic-slice_fusion.2
  57.3 0.8 fusion.45
  58.2 0.7 bitcast_dynamic-update-slice_fusion.2
  58.9 0.7 constant_dynamic-slice_fusion.2
  59.6 0.8 fusion.45
  60.5 0.7 bitcast_dynamic-update-slice_fusion.2
  61.1 0.7 constant_dynamic-slice_fusion.2
  61.8 0.8 fusion.45
  62.7 0.7 bitcast_dynamic-update-slice_fusion.2
  63.4 0.7 constant_dynamic-slice_fusion.2
  64.1 0.8 fusion.45
  65.0 0.7 bitcast_dynamic-update-slice_fusion.2
  65.7 0.7 constant_dynamic-slice_fusion.2
  66.4 0.8 fusion.45
  67.2 0.7 bitcast_dynamic-update-slice_fusion.2
  67.9 0.7 constant_dynamic-slice_fusion.2
  68.6 0.8 fusion.45
  69.5 0.7 bitcast_dynamic-update-slice_fusion.2
  70.2 2.0 %reshape.100 = f32[16,5,16,256]{3,2,1,0:T(8,128)S(1)} reshape(f32[16,5,4096]{2,1,0:T(8,128)} %get-tuple-element.29) | data formatting | bytes 2621440 | tf_op jit(solution)/shard_map/reshape | solution.py:11
  72.2 1.8 %copy.54 = f32[16,16,5,256]{3,1,2,0:T(8,128)} copy(f32[16,16,5,256]{3,0,2,1:T(8,128)S(1)} %bitcast.76) | data formatting | bytes 2621440 | tf_op jit(solution)/shard_map/transpose | solution.py:11
  74.0 8.2 %all-to-all-start = ((f32[16,16,5,256]{3,1,2,0:T(8,128)}), f32[16,16,5,256]{3,1,2,0:T(8,128)S(1)}, u32[]{:S(2)}, u32[]{:S(2)}) async-start(f32[16,16,5,256]{3,1,2,0:T(8,128)} %copy.54), calls=%async_computation | async-start | bytes 2621440 | tf_op jit(solution)/shard_map/all_to_all | solution.py:16
  82.2 20.9 %all-to-all-done = f32[16,16,5,256]{3,1,2,0:T(8,128)S(1)} async-done(((f32[16,16,5,256]{3,1,2,0:T(8,128)}), f32[16,16,5,256]{3,1,2,0:T(8,128)S(1)}, u32[]{:S(2)}, u32[]{:S(2)}) %all-to-all-start) | async-done | bytes 1310752 | tf_op jit(solution)/shard_map/all_to_all | solution.py:16
  103.2 13.6 %all-gather = f32[128,5,256]{2,0,1:T(8,128)S(1)} all-gather(f32[16,5,256]{2,0,1:T(8,128)S(1)} %reduce_sum.54), channel_id=2, replica_groups=mesh['gx'=4,'gy'=4,'gz'=8] {'gz'}, dimensions={0}, use_global_device_ids=true | all-gather | bytes 737280 | tf_op jit(solution)/shard_map/all_gather | solution.py:21
  117.6 3.5 %all-to-all-start.2 = ((f32[16,1,16]{2,1,0:T(1,128)}), f32[16,1,16]{2,1,0:T(1,128)S(1)}, u32[]{:S(2)}, u32[]{:S(2)}) async-start(f32[16,1,16]{2,1,0:T(1,128)} %broadcast_in_dim.39), calls=%async_computation.2 | async-start | bytes 16384 | tf_op jit(solution)/shard_map/all_to_all | solution.py:27
  122.3 6.3 %all-to-all-done.2 = f32[16,1,16]{2,1,0:T(1,128)S(1)} async-done(((f32[16,1,16]{2,1,0:T(1,128)}), f32[16,1,16]{2,1,0:T(1,128)S(1)}, u32[]{:S(2)}, u32[]{:S(2)}) %all-to-all-start.2) | async-done | bytes 1056 | tf_op jit(solution)/shard_map/all_to_all | solution.py:27
  128.5 0.7 broadcast_in_dim.24
  129.3 3.4 %all-to-all-start.1 = ((f32[4,16,4,256]{3,2,1,0:T(4,128)}), f32[4,16,4,256]{3,2,1,0:T(4,128)S(1)}, u32[]{:S(2)}, u32[]{:S(2)}) async-start(f32[4,16,4,256]{3,2,1,0:T(4,128)} %broadcast_in_dim.24), calls=%async_computation.1 | async-start | bytes 524288 | tf_op jit(solution)/shard_map/all_to_all | solution.py:27
  133.1 9.0 %all-reduce.1 = (f32[16,5]{0,1:T(8,128)S(1)}, f32[16]{0:T(128)S(1)}) all-reduce(f32[16,5]{0,1:T(8,128)S(1)} %reduce_sum.58, f32[16]{0:T(128)S(1)} %fusion.28), channel_id=1, replica_groups=mesh['gx'=4,'gy'=4,'gz'=8] {'gx'}, use_global_device_ids=true, to_apply=%region_12.13 | all-reduce | flops 96 | bytes 768 | tf_op jit(solution)/shard_map/psum | solution.py:54
  142.1 11.0 %all-reduce = (f32[16,5]{0,1:T(8,128)S(1)}, f32[16]{0:T(128)S(1)}) all-reduce(f32[16,5]{0,1:T(8,128)S(1)} %get-tuple-element.54, f32[16]{0:T(128)S(1)} %get-tuple-element.55), channel_id=1, replica_groups=mesh['gx'=4,'gy'=4,'gz'=8] {'gy'}, use_global_device_ids=true, to_apply=%region_13.14 | all-reduce | flops 96 | bytes 768 | tf_op jit(solution)/shard_map/psum | solution.py:54
  153.8 0.7 copy.66
  (107 shorter events, 5.2 us)
Async XLA Ops:
  0.6 1.6 %copy-start = (bf16[1024,1024]{1,0:T(8,128)(2,1)S(1)}, bf16[1024,1024]{1,0:T(8,128)(2,1)}, u32[]{:S(2)}) copy-start(bf16[1024,1024]{1,0:T(8,128)(2,1)} %param.18) | copy-start | bytes 6291460
  2.2 18.6 %copy-start.3 = (bf16[1024,512]{1,0:T(8,128)(2,1)S(1)}, bf16[1024,512]{1,0:T(8,128)(2,1)}, u32[]{:S(2)}) copy-start(bf16[1024,512]{1,0:T(8,128)(2,1)} %param.20) | copy-start | bytes 3145732
  2.2 18.6 %copy-start.4 = (bf16[512,256]{1,0:T(8,128)(2,1)S(1)}, bf16[512,256]{1,0:T(8,128)(2,1)}, u32[]{:S(2)}) copy-start(bf16[512,256]{1,0:T(8,128)(2,1)} %param.22) | copy-start | bytes 786436
  2.2 18.6 %copy-start.5 = (f32[1024]{0:T(1024)S(1)}, f32[1024]{0:T(1024)}, u32[]{:S(2)}) copy-start(f32[1024]{0:T(1024)} %param.19) | copy-start | bytes 12292
  2.2 18.6 %copy-start.6 = (f32[512]{0:T(512)S(1)}, f32[512]{0:T(512)}, u32[]{:S(2)}) copy-start(f32[512]{0:T(512)} %param.21) | copy-start | bytes 6148
  2.3 18.6 %copy-start.7 = (f32[256]{0:T(256)S(1)}, f32[256]{0:T(256)}, u32[]{:S(2)}) copy-start(f32[256]{0:T(256)} %param.23) | copy-start | bytes 3076
  20.9 10.5 %copy-start.2 = (bf16[256,1]{0,1:T(2,128)(2,1)S(1)}, bf16[256,1]{0,1:T(2,128)(2,1)}, u32[]{:S(2)}) copy-start(bf16[256,1]{0,1:T(2,128)(2,1)} %param.24) | copy-start | bytes 1540
  20.9 12.8 %copy-start.1 = (s32[16,256]{1,0:T(8,128)S(1)}, s32[16,256]{1,0:T(8,128)}, u32[]{:S(2)}) copy-start(s32[16,256]{1,0:T(8,128)} %param.27) | copy-start | bytes 49156
  74.0 29.1 %all-to-all-start = ((f32[16,16,5,256]{3,1,2,0:T(8,128)}), f32[16,16,5,256]{3,1,2,0:T(8,128)S(1)}, u32[]{:S(2)}, u32[]{:S(2)}) async-start(f32[16,16,5,256]{3,1,2,0:T(8,128)} %copy.54), calls=%async_computation | async-start | bytes 2621440 | tf_op jit(solution)/shard_map/all_to_all | solution.py:16
  117.6 10.9 %all-to-all-start.2 = ((f32[16,1,16]{2,1,0:T(1,128)}), f32[16,1,16]{2,1,0:T(1,128)S(1)}, u32[]{:S(2)}, u32[]{:S(2)}) async-start(f32[16,1,16]{2,1,0:T(1,128)} %broadcast_in_dim.39), calls=%async_computation.2 | async-start | bytes 16384 | tf_op jit(solution)/shard_map/all_to_all | solution.py:27
  129.3 24.5 %all-to-all-start.1 = ((f32[4,16,4,256]{3,2,1,0:T(4,128)}), f32[4,16,4,256]{3,2,1,0:T(4,128)S(1)}, u32[]{:S(2)}, u32[]{:S(2)}) async-start(f32[4,16,4,256]{3,2,1,0:T(4,128)} %broadcast_in_dim.24), calls=%async_computation.1 | async-start | bytes 524288 | tf_op jit(solution)/shard_map/all_to_all | solution.py:27
where the time goes:
time: 156 us; the launch traced here: 154 us
  matrix products  44.1 us (28%)
  blocking collectives  33.6 us (22%)
  local copies, waits for them, and re-layouts  29.8 us (19%)
  waiting for transfers between devices  27.2 us (17%)
  starting transfers between devices  15 us (10%)
  other arithmetic  2.68 us (2%)
  between operations  1.7 us (1%)
    dot_general x2, matrix products, layer_relu(): jnp.dot(inputs, weight, preferred_element_type=jnp.float32) + offset  29.1 us
    all_to_all x1, waiting for transfers between devices, sent_and_summed(): lax.all_to_all(tiles, axis, split_axis=0, concat_axis=0, tiled=True)  20.9 us
    psum x2, blocking collectives, one_axis_at_a_time(): value = lax.psum(value, axis)  20 us
    all_gather x1, blocking collectives, gathered_total(): tiles = lax.all_gather(value, axis)  13.6 us
    dot_general x16, matrix products, histogram_one(): partial_value = jnp.dot(parts, one_hot, preferred_element_type=jnp.float32)  12.8 us
    dynamic_slice x16, local copies, waits for them, and re-layouts, on_device(): histograms = lax.map(histogram_one, (values, bucket_index))  11.2 us
    dynamic_update_slice x16, local copies, waits for them, and re-layouts, on_device(): histograms = lax.map(histogram_one, (values, bucket_index))  10.6 us
    all_to_all x1, starting transfers between devices, sent_and_summed(): lax.all_to_all(tiles, axis, split_axis=0, concat_axis=0, tiled=True)  8.16 us
  transfers between devices with their start and end apart: 3, of which 2 were waited for; matrix products, arithmetic and copies ran while one was open for 1% of the time, Pallas kernels for 0%

commit v1 on v0

v1 whole, which is shorter than its diff:
```python
import jax
import jax.numpy as jnp
from jax import lax
from jax.experimental import pallas as pl
from jax.experimental.pallas import tpu as pltpu
from jax.sharding import PartitionSpec as P

NBUCK = 4096
RANGE = 512
LOW = 64
HIGH = RANGE // LOW
ALL = ("gx", "gy", "gz")
ROWS_PER_STEP = 1024
PAYLOAD = 4 * RANGE + 128


def mlp_body(x, w1, b1, w2, b2, w3, b3, w4, b4, wo, bo, out):
    intervals = x.shape[0]
    rows = intervals * x.shape[1]
    chains = 4
    flat = x[...].reshape(rows, x.shape[2])
    size = rows // chains
    hidden = [flat[c * size : (c + 1) * size] for c in range(chains)]
    for w, b in ((w1, b1), (w2, b2), (w3, b3), (w4, b4)):
        hidden = [
            jnp.maximum(
                jnp.dot(h, w[...], preferred_element_type=jnp.float32) + b[...], 0.0
            ).astype(jnp.bfloat16)
            for h in hidden
        ]
    last = jnp.concatenate(hidden, axis=0)
    logits = (
        lax.dot_general(
            wo[...], last, (((1,), (1,)), ((), ())), preferred_element_type=jnp.float32
        )
        + bo[0]
    )
    per = x.shape[1]
    for i in range(intervals):
        row = logits[0:1, i * per : (i + 1) * per]
        for a in range(out.shape[0]):
            for c in range(out.shape[2]):
                out[a, i, c] = row


def mlp_logits(x, w1, b1, w2, b2, w3, b3, w4, b4, wo, bo, copies):
    intervals, per, _ = x.shape
    step = ROWS_PER_STEP // per
    before, after = copies
    whole = lambda a: pl.BlockSpec(a.shape, lambda i: (0,) * a.ndim)
    biases = [b.reshape(1, -1) for b in (b1, b2, b3, b4)]
    out_row = jnp.broadcast_to(wo.reshape(1, -1), (16, wo.shape[0]))
    ops = []
    for w, b in zip((w1, w2, w3, w4), biases):
        ops += [w, b]
    ops.append(out_row)
    return pl.pallas_call(
        mlp_body,
        grid=(intervals // step,),
        in_specs=[pl.BlockSpec((step, per, x.shape[2]), lambda i: (i, 0, 0))]
        + [whole(a) for a in ops]
        + [pl.BlockSpec(memory_space=pltpu.SMEM)],
        out_specs=pl.BlockSpec((before, step, after, 1, per), lambda i: (0, i, 0, 0, 0)),
        out_shape=jax.ShapeDtypeStruct((before, intervals, after, 1, per), jnp.float32),
        compiler_params=pltpu.CompilerParams(
            dimension_semantics=("arbitrary",), vmem_limit_bytes=56 * 2**20
        ),
        name="mlp",
    )(x, *ops, bo)


def one_hot_rows(index_row, count):
    rows = lax.broadcasted_iota(jnp.int32, (count, index_row.shape[1]), 0)
    return jnp.where(rows == index_row, 1.0, 0.0).astype(jnp.bfloat16)


def nt_dot(a, b):
    return lax.dot_general(a, b, (((1,), (1,)), ((), ())), preferred_element_type=jnp.float32)


def count_body(block, tags, rate, inverse, numerator, acc):
    sources = tags.shape[0]
    per = tags.shape[2] // 2
    group = 8
    acc[...] = jnp.zeros_like(acc)

    def step(g, carry):
        left, right = [], []
        for k in range(group):
            row = tags[g * group + k]
            bucket, label = row[:, :per], row[:, per:]
            digit = lax.shift_right_logical(bucket, 7) + 32 * (1 - label)
            left.append(one_hot_rows(digit, 64))
            right.append(one_hot_rows(jnp.bitwise_and(bucket, 127), 128))
        acc[...] += nt_dot(jnp.concatenate(left, 1), jnp.concatenate(right, 1))
        return carry

    lax.fori_loop(0, sources // group, step, 0)
    pos, neg = acc[0:32], acc[32:64]
    lane = lax.broadcasted_iota(jnp.int32, neg.shape, 1)
    sub = lax.broadcasted_iota(jnp.int32, neg.shape, 0)
    run = neg
    for shift in (1, 2, 4, 8, 16, 32, 64):
        run = run + jnp.where(lane >= shift, pltpu.roll(run, shift, 1), 0.0)
    total = jnp.broadcast_to(jnp.sum(neg, axis=1, keepdims=True), neg.shape)
    above = total
    for shift in (1, 2, 4, 8, 16):
        above = above + jnp.where(sub >= shift, pltpu.roll(above, shift, 0), 0.0)
    below = run - neg + above - total
    pairs = jnp.sum(pos * (below + 0.5 * neg))
    positives, negatives = jnp.sum(pos), jnp.sum(neg)
    pick = lax.broadcasted_iota(jnp.int32, (1, 128), 1)
    numerator[...] = jnp.where(
        pick == 0,
        pairs / jnp.maximum(positives * negatives, 1.0),
        jnp.where(
            pick == 2,
            1.0 / jnp.maximum(positives, 1.0),
            1.0 / jnp.maximum(positives + negatives, 1.0),
        ),
    )
    first = block[0] * 4
    own_pos, own_neg = acc[pl.ds(first, 4)], acc[pl.ds(first + 32, 4)]
    count = jnp.maximum(own_pos + own_neg, 1.0)
    rate[...] = own_pos / count
    inverse[...] = 1.0 / count


def value_body(block, tags, logits, rate, inverse, numerator, out, parts, digits):
    sources = tags.shape[0]
    per = logits.shape[2]
    z = logits[:, 0, :]
    bucket = tags[:, 0, :per]
    y = tags[:, 0, per:].astype(jnp.float32)
    p = jax.nn.sigmoid(z)
    loss = jax.nn.softplus(z) - y * z
    sq = (p - y) ** 2
    sums = []
    for v, value in enumerate((p, loss, sq)):
        upper = value.astype(jnp.bfloat16).astype(jnp.float32)
        parts[2 * v] = upper
        parts[2 * v + 1] = value - upper
        sums.append(jnp.sum(value))
    digits[0] = lax.shift_right_arithmetic(bucket - block[0] * RANGE, 6)
    digits[1] = jnp.bitwise_and(bucket, LOW - 1)
    group = 8

    def step(g, acc):
        left, right = [], []
        for k in range(group):
            i = g * group + k
            high = digits[0, pl.ds(i, 1), :]
            match = lax.broadcasted_iota(jnp.int32, (HIGH, per), 0) == high
            left.append(
                jnp.concatenate(
                    [jnp.where(match, parts[v, pl.ds(i, 1), :], 0.0) for v in range(6)], 0
                ).astype(jnp.bfloat16)
            )
            right.append(one_hot_rows(digits[1, pl.ds(i, 1), :], LOW))
        return acc + nt_dot(jnp.concatenate(left, 1), jnp.concatenate(right, 1))

    acc = lax.fori_loop(0, sources // group, step, jnp.zeros((6 * HIGH, LOW), jnp.float32))
    rows = [rate[...]]
    for v in range(3):
        both = acc[2 * v * HIGH : (2 * v + 1) * HIGH] + acc[(2 * v + 1) * HIGH : (2 * v + 2) * HIGH]
        rows.append(
            jnp.concatenate(
                [
                    jnp.concatenate([both[2 * t : 2 * t + 1], both[2 * t + 1 : 2 * t + 2]], 1)
                    for t in range(HIGH // 2)
                ],
                0,
            )
            * inverse[...]
        )
    copies = out.shape[0]
    for t in range(HIGH // 2):
        for r in range(4):
            at = (t * 4 + r) * 128
            out[:, 0, at : at + 128] = jnp.broadcast_to(rows[r][t : t + 1], (copies, 128))
    pick = lax.broadcasted_iota(jnp.int32, (1, 128), 1)
    scale = numerator[...]
    last = jnp.where(
        pick == 0,
        scale,
        scale * jnp.where(pick == 1, sums[1], jnp.where(pick == 2, sums[0], sums[2])),
    )
    out[:, 0, 4 * RANGE :] = jnp.broadcast_to(last, (copies, 128))


def call_counts(block, tags):
    vmem = pl.BlockSpec(memory_space=pltpu.VMEM)
    return pl.pallas_call(
        count_body,
        in_specs=[pl.BlockSpec(memory_space=pltpu.SMEM), vmem],
        out_specs=[vmem] * 3,
        out_shape=[
            jax.ShapeDtypeStruct((4, 128), jnp.float32),
            jax.ShapeDtypeStruct((4, 128), jnp.float32),
            jax.ShapeDtypeStruct((1, 128), jnp.float32),
        ],
        scratch_shapes=[pltpu.VMEM((64, 128), jnp.float32)],
        name="counts",
    )(block, tags)


def call_values(block, tags, logits, rate, inverse, numerator, copies):
    vmem = pl.BlockSpec(memory_space=pltpu.VMEM)
    sources, _, per = logits.shape
    return pl.pallas_call(
        value_body,
        in_specs=[pl.BlockSpec(memory_space=pltpu.SMEM)] + [vmem] * 5,
        out_specs=vmem,
        out_shape=jax.ShapeDtypeStruct((copies, 1, PAYLOAD), jnp.float32),
        scratch_shapes=[
            pltpu.VMEM((6, sources, per), jnp.float32),
            pltpu.VMEM((2, sources, per), jnp.int32),
        ],
        name="values",
    )(block, tags, logits, rate, inverse, numerator)


def on_device(
    interact,
    weight_one,
    bias_one,
    weight_two,
    bias_two,
    weight_three,
    bias_three,
    weight_four,
    bias_four,
    weight_out,
    bias_out,
    bucket_index,
    labels,
):
    intervals, per, _ = interact.shape
    sizes = [lax.axis_size(a) for a in ALL]
    everyone = sizes[0] * sizes[1] * sizes[2]
    before, after = sizes[0], 2
    tags = jnp.concatenate([bucket_index, labels], axis=1)
    tags = jnp.broadcast_to(
        tags[None, :, None, None], (before, intervals, after, 1, 2 * per)
    ).reshape(everyone, 1, 2 * per)
    tags = lax.all_to_all(tags, ALL, 0, 0, tiled=True)
    block = (lax.axis_index("gx") * 2 + lax.axis_index("gz") % 2).reshape(1).astype(jnp.int32)
    logits = mlp_logits(
        interact,
        weight_one,
        bias_one,
        weight_two,
        bias_two,
        weight_three,
        bias_three,
        weight_four,
        bias_four,
        weight_out,
        bias_out,
        (before, after),
    ).reshape(everyone, 1, per)
    logits = lax.all_to_all(logits, ALL, 0, 0, tiled=True)
    rate, inverse, numerator = call_counts(block, tags)
    group = sizes[1] * sizes[2]
    payload = call_values(block, tags, logits, rate, inverse, numerator, group)
    payload = lax.all_to_all(payload, ("gy", "gz"), 0, 0, tiled=True)
    payload = payload.reshape(intervals, after, PAYLOAD)
    reports = payload[:, :, : 4 * RANGE].reshape(intervals, after, RANGE // 128, 4, 128)
    reports = reports.transpose(0, 3, 1, 2, 4).reshape(intervals, 4, after * RANGE)
    return reports, payload[:, 0, 4 * RANGE : 4 * RANGE + 4]


def solution(mesh):
    split = P(None, ALL)
    in_specs = (P(None, ALL, None),) + (P(),) * 10 + (split, split)
    out_specs = (P(None, None, "gx"), P())
    return jax.shard_map(
        on_device, mesh=mesh, in_specs=in_specs, out_specs=out_specs, check_vma=False
    )
```

time: 156 us -> 83.9 us (0.54)
  the two profiles are of different devices: /device:TPU:0 before, /device:TPU:1 now
where the time goes in v1:
time: 83.9 us; the launch traced here: 83.5 us
  Pallas kernels  37.8 us (45%)
  starting transfers between devices  21.3 us (25%)
  blocking collectives  13.6 us (16%)
  local copies, waits for them, and re-layouts  4.48 us (5%)
  waiting for transfers between devices  2.8 us (3%)
  other arithmetic  2.09 us (2%)
  between operations  1.37 us (2%)
    pallas_call x1, Pallas kernels, mlp_logits(): pl.pallas_call(mlp_body, grid=(intervals // step,), in_specs=[pl.BlockSpe...  23 us
    all_to_all x1, blocking collectives, on_device(): payload = lax.all_to_all(payload, ('gy', 'gz'), 0, 0, tiled=True)  13.6 us
    all_to_all x1, starting transfers between devices, on_device(): tags = lax.all_to_all(tags, ALL, 0, 0, tiled=True)  11.5 us
    all_to_all x1, starting transfers between devices, on_device(): logits = lax.all_to_all(logits, ALL, 0, 0, tiled=True)  9.77 us
    pallas_call x1, Pallas kernels, call_values(): pl.pallas_call(value_body, in_specs=[pl.BlockSpec(memory_space=pltpu.SMEM...  7.65 us
    pallas_call x1, Pallas kernels, call_counts(): pl.pallas_call(count_body, in_specs=[pl.BlockSpec(memory_space=pltpu.SMEM...  7.19 us
    all_to_all x1, waiting for transfers between devices, on_device(): logits = lax.all_to_all(logits, ALL, 0, 0, tiled=True)  2.8 us
  transfers between devices with their start and end apart: 2, of which 1 were waited for; matrix products, arithmetic and copies ran while one was open for 2% of the time, Pallas kernels for 36%

profile of v1, /device:TPU:1, one launch (start us, length us, event | category | flops | bytes accessed | tf_op | source)
XLA Modules:
  0.0 83.5 jit_solution(11612618416519735881)
XLA Ops:
  0.6 0.7 pad_add_fusion
  1.4 0.1 broadcast_in_dim.15
  1.4 1.1 %broadcast_in_dim.16 = s32[128,1,512]{2,1,0:T(1,128)} reshape(s32[4,16,2,512]{3,2,1,0:T(2,128)S(1)} %broadcast_in_dim.15) | data formatting | bytes 524288 | tf_op jit(solution)/shard_map/broadcast_in_dim | solution.py:243
  2.6 11.5 %all-to-all-start = ((s32[128,1,512]{2,1,0:T(1,128)}), s32[128,1,512]{2,1,0:T(1,128)S(1)}, u32[]{:S(2)}, u32[]{:S(2)}) async-start(s32[128,1,512]{2,1,0:T(1,128)} %broadcast_in_dim.16), calls=%async_computation | async-start | bytes 524288 | tf_op jit(solution)/shard_map/all_to_all | solution.py:246
  14.7 0.7 reduce
  15.4 0.6 broadcast_in_dim.18.wo
  16.0 23.0 %mlp.1 = f32[4,16,2,1,256]{4,3,2,1,0:T(1,128)} custom-call(bf16[16,256,512]{2,1,0:T(8,128)(2,1)} %x.1, bf16[512,1024]{1,0:T(8,128)(2,1)} %w1.1, f32[1,1024]{1,0:T(1,128)} %bitcast.12, bf16[1024,1024]{1,0:T(8,128)(2,1)} %w2.1, f32[1,1024]{1,0:T(1,128)} %bitcast.13, bf16[1024,512]{1,0:T(8,128)(2,1)} %w3.1, f32[1,512]{1,0:T(1,128)} %bitcast.15, ...), custom_call_target="tpu_custom_call" | custom-call | tf_op jit(solution)/shard_map/mlp/pallas_call | solution.py:57
  39.0 0.0 all-to-all-done.tags
  39.0 0.0 copy-start
  39.0 9.8 %all-to-all-start.1 = ((f32[128,1,256]{2,1,0:T(1,128)}), f32[128,1,256]{2,1,0:T(1,128)S(1)}, u32[]{:S(2)}, u32[]{:S(2)}) async-start(f32[128,1,256]{2,1,0:T(1,128)} %bitcast.11), calls=%async_computation.1 | async-start | bytes 262144 | tf_op jit(solution)/shard_map/all_to_all | solution.py:262
  48.8 0.0 copy-done
  48.8 7.2 %counts.1 = (f32[4,128]{1,0:T(4,128)}, f32[4,128]{1,0:T(4,128)}, f32[1,128]{1,0:T(1,128)}) custom-call(s32[1]{0:T(128)} %bitcast.block, s32[128,1,512]{2,1,0:T(1,128)} %copy-done), custom_call_target="tpu_custom_call" | custom-call | tf_op jit(solution)/shard_map/counts/pallas_call | solution.py:193
  56.0 2.8 %all-to-all-done.1.logits = f32[128,1,256]{2,1,0:T(1,128)S(1)} async-done(((f32[128,1,256]{2,1,0:T(1,128)}), f32[128,1,256]{2,1,0:T(1,128)S(1)}, u32[]{:S(2)}, u32[]{:S(2)}) %all-to-all-start.1) | async-done | bytes 131104 | tf_op jit(solution)/shard_map/all_to_all | solution.py:262
  58.8 0.0 copy-start.1
  58.8 0.7 copy-done.1
  59.5 7.7 %values.1 = f32[32,1,2176]{2,1,0:T(1,128)} custom-call(s32[1]{0:T(128)} %bitcast.block, s32[128,1,512]{2,1,0:T(1,128)} %copy-done, f32[128,1,256]{2,1,0:T(1,128)} %copy-done.1, f32[4,128]{1,0:T(4,128)} %get-tuple-element.5.rate, f32[4,128]{1,0:T(4,128)} %get-tuple-element.6.inverse, f32[1,128]{1,0:T(1,128)} %get-tuple-element.7.numerator), custom_call_target="tpu_custom_call" | custom-call | tf_op jit(solution)/shard_map/values/pallas_call | solution.py:210
  67.1 13.6 %all_to_all.15 = f32[32,1,2176]{2,1,0:T(1,128)S(1)} all-to-all(f32[32,1,2176]{2,1,0:T(1,128)} %values.1), channel_id=1, replica_groups=mesh['gx'=4,'gy'=4,'gz'=8] {'gy','gz'}, dimensions={0} | all-to-all | bytes 557056 | tf_op jit(solution)/shard_map/all_to_all | solution.py:266
  80.7 0.7 reduce.1
  81.4 0.2 reshape.46
  81.6 0.7 copy.18
  82.2 0.3 reshape.47
  82.5 0.1 copy.20
  82.6 0.9 %reshape.48 = f32[16,4,1024]{2,1,0:T(4,128)} reshape(f32[16,4,2,4,128]{4,3,2,1,0:T(4,128)S(1)} %bitcast.10) | data formatting | bytes 524288 | tf_op jit(solution)/shard_map/reshape | solution.py:269
  (2 shorter events, 0.0 us)
Async XLA Ops:
  2.6 36.4 %all-to-all-start = ((s32[128,1,512]{2,1,0:T(1,128)}), s32[128,1,512]{2,1,0:T(1,128)S(1)}, u32[]{:S(2)}, u32[]{:S(2)}) async-start(s32[128,1,512]{2,1,0:T(1,128)} %broadcast_in_dim.16), calls=%async_computation | async-start | bytes 524288 | tf_op jit(solution)/shard_map/all_to_all | solution.py:246
  39.0 9.8 %copy-start = (s32[128,1,512]{2,1,0:T(1,128)}, s32[128,1,512]{2,1,0:T(1,128)S(1)}, u32[]{:S(2)}) copy-start(s32[128,1,512]{2,1,0:T(1,128)S(1)} %all-to-all-done.tags) | copy-start | bytes 786436
  39.0 19.8 %all-to-all-start.1 = ((f32[128,1,256]{2,1,0:T(1,128)}), f32[128,1,256]{2,1,0:T(1,128)S(1)}, u32[]{:S(2)}, u32[]{:S(2)}) async-start(f32[128,1,256]{2,1,0:T(1,128)} %bitcast.11), calls=%async_computation.1 | async-start | bytes 262144 | tf_op jit(solution)/shard_map/all_to_all | solution.py:262
  58.8 0.7 copy-start.1

commit v2 on v0

v2 whole, which is shorter than its diff:
```python
import jax
import jax.numpy as jnp
from jax import lax
from jax.experimental import pallas as pl
from jax.experimental.pallas import tpu as pltpu
from jax.sharding import PartitionSpec as P

RANGE = 512
LOW = 128
OWN = RANGE // LOW
HIGH = 4096 // LOW
ALL = ("gx", "gy", "gz")
REPORT = 4 * RANGE
PAYLOAD = REPORT + 128
BF16 = jnp.bfloat16
F32 = jnp.float32


def in_vmem(value):
    return pltpu.with_memory_space_constraint(value, pltpu.VMEM)


def nt_dot(a, b):
    return lax.dot_general(a, b, (((1,), (1,)), ((), ())), preferred_element_type=F32)


def mlp_body(steps, chains, sources, bo, out, held, sem):
    x, buckets, labels = held[:3]
    intervals, per, width = x.shape
    each = intervals // steps
    copies = [
        pltpu.make_async_copy(src, dst, sem.at[steps + k])
        for k, (src, dst) in enumerate(zip(sources[1:], held[1:]))
    ]
    tags, weights, last_weight = copies[:2], copies[2:-1], copies[-1]
    feeds = []
    for k in range(steps):
        part = pl.ds(k * each, each)
        feeds.append(pltpu.make_async_copy(sources[0].at[part], x.at[part], sem.at[k]))
    for copy in feeds[:1] + weights + [last_weight] + tags + feeds[1:]:
        copy.start()

    def run(k, waiting):
        if waiting:
            feeds[0].wait()
        flat = x[pl.ds(k * each, each)].reshape(each * per, width)
        size = each * per // chains
        hidden = [flat[c * size : (c + 1) * size] for c in range(chains)]
        for j in range(4):
            w, b = held[3 + 2 * j], held[4 + 2 * j]
            if waiting:
                weights[2 * j].wait()
                weights[2 * j + 1].wait()
            hidden = [
                jnp.maximum(jnp.dot(h, w[...], preferred_element_type=F32) + b[...], 0.0).astype(
                    BF16
                )
                for h in hidden
            ]
        if waiting:
            for copy in [last_weight] + tags:
                copy.wait()
        column = jnp.broadcast_to(held[-1][...], (16, held[-1].shape[1]))
        logits = nt_dot(column, jnp.concatenate(hidden, axis=0)) + bo[0]
        for i in range(each):
            at = k * each + i
            row = jnp.concatenate(
                [
                    buckets[pl.ds(at, 1), :].astype(F32),
                    labels[pl.ds(at, 1), :].astype(F32),
                    logits[0:1, i * per : (i + 1) * per],
                ],
                axis=1,
            )
            for a in range(out.shape[0]):
                for c in range(out.shape[2]):
                    out[a, at, c] = row

    run(0, True)
    for copy in feeds[1:]:
        copy.wait()

    def step(k, carry):
        run(k, False)
        return carry

    lax.fori_loop(1, steps, step, 0)


def examples_to_send(x, buckets, labels, weights, biases, wo, bo, copies):
    intervals, per, _ = x.shape
    steps, chains = 4, 4
    before, after = copies
    ops = [x, buckets, labels]
    for w, b in zip(weights, biases):
        ops += [w, b.reshape(1, -1)]
    ops.append(wo.T)
    count = len(ops)

    def body(*refs):
        mlp_body(
            steps,
            chains,
            refs[:count],
            refs[count],
            refs[count + 1],
            refs[count + 2 : -1],
            refs[-1],
        )

    return pl.pallas_call(
        body,
        in_specs=[pl.BlockSpec(memory_space=pltpu.HBM)] * count
        + [pl.BlockSpec(memory_space=pltpu.SMEM)],
        out_specs=pl.BlockSpec(memory_space=pltpu.VMEM),
        out_shape=pltpu.VMEM((before, intervals, after, 1, 3 * per), F32),
        scratch_shapes=[pltpu.VMEM(a.shape, a.dtype) for a in ops]
        + [pltpu.SemaphoreType.DMA((steps + count - 1,))],
        compiler_params=pltpu.CompilerParams(vmem_limit_bytes=40 * 2**20),
        name="mlp",
    )(*[pltpu.with_memory_space_constraint(a, pltpu.HBM) for a in ops], bo)


def one_hot_rows(row, iota):
    wide = jnp.broadcast_to(row, (16, row.shape[1])).astype(BF16)
    one, zero = jnp.ones((), BF16), jnp.zeros((), BF16)
    return jnp.concatenate(
        [jnp.where(iota[k : k + 16] == wide, one, zero) for k in range(0, iota.shape[0], 16)], 0
    )


def histogram_body(rec, out, vals, digits, acc):
    sources = rec.shape[0]
    per = rec.shape[2] // 3
    group = 32
    block = lax.axis_index("gx") * 2 + lax.axis_index("gz") % 2
    bucket = rec[:, 0, :per].astype(jnp.int32)
    y = rec[:, 0, per : 2 * per]
    z = rec[:, 0, 2 * per :]
    p = jax.nn.sigmoid(z)
    loss = jax.nn.softplus(z) - y * z
    sq = (p - y) ** 2
    sums = []
    for v, value in enumerate((p, loss, sq)):
        upper = value.astype(BF16).astype(F32)
        vals[:, 2 * v, :] = upper
        vals[:, 2 * v + 1, :] = value - upper
        sums.append(jnp.sum(value))
    vals[:, 6, :] = jnp.zeros_like(y)
    vals[:, 7, :] = jnp.zeros_like(y)
    high = lax.shift_right_logical(bucket, 7)
    digits[0] = (high + jnp.where(y > 0.5, 0, HIGH)).astype(F32)
    digits[1] = jnp.bitwise_and(bucket, LOW - 1).astype(F32)
    digits[2] = (high - block * OWN).astype(F32)
    iota_high = lax.broadcasted_iota(jnp.int32, (2 * HIGH, per), 0).astype(F32).astype(BF16)
    iota_low = lax.broadcasted_iota(jnp.int32, (LOW, per), 0).astype(F32).astype(BF16)

    def step(g, carry):
        left, right = [], []
        for k in range(group):
            i = g * group + k
            own = jnp.broadcast_to(digits[2, pl.ds(i, 1), :], (8, per))
            mine = jnp.concatenate(
                [jnp.where(own == float(h), vals[i], 0.0) for h in range(OWN)], 0
            ).astype(BF16)
            counts = one_hot_rows(digits[0, pl.ds(i, 1), :], iota_high)
            left.append(jnp.concatenate([counts, mine], 0))
            right.append(one_hot_rows(digits[1, pl.ds(i, 1), :], iota_low))
        return carry + nt_dot(jnp.concatenate(left, 1), jnp.concatenate(right, 1))

    total = jnp.zeros((2 * HIGH + 8 * OWN, LOW), F32)
    total = lax.fori_loop(0, sources // group, step, total)
    acc[...] = total
    pos, neg = total[:HIGH], total[HIGH : 2 * HIGH]
    lane = lax.broadcasted_iota(jnp.int32, neg.shape, 1)
    sub = lax.broadcasted_iota(jnp.int32, neg.shape, 0)
    run = neg
    for shift in (1, 2, 4, 8, 16, 32, 64):
        run = run + jnp.where(lane >= shift, pltpu.roll(run, shift, 1), 0.0)
    line = jnp.broadcast_to(jnp.sum(neg, axis=1, keepdims=True), neg.shape)
    above = line
    for shift in (1, 2, 4, 8, 16):
        above = above + jnp.where(sub >= shift, pltpu.roll(above, shift, 0), 0.0)
    below = run - neg + above - line
    pairs = jnp.sum(pos * (below + 0.5 * neg))
    positives, negatives = jnp.sum(pos), jnp.sum(neg)
    first = block * OWN
    own_pos, own_neg = acc[pl.ds(first, OWN)], acc[pl.ds(first + HIGH, OWN)]
    inverse = 1.0 / jnp.maximum(own_pos + own_neg, 1.0)
    copies = out.shape[0]
    for t in range(OWN):
        scale = inverse[t : t + 1]
        for r in range(4):
            at = 2 * HIGH + 8 * t + 2 * (r - 1)
            sum_row = total[at : at + 1] + total[at + 1 : at + 2] if r else own_pos[t : t + 1]
            to = (t * 4 + r) * LOW
            out[:, 0, to : to + LOW] = jnp.broadcast_to(sum_row * scale, (copies, LOW))
    pick = lax.broadcasted_iota(jnp.int32, (1, 128), 1)
    upper_part = jnp.where(
        pick == 0, pairs, jnp.where(pick == 1, sums[1], jnp.where(pick == 2, sums[0], sums[2]))
    )
    lower_part = jnp.where(
        pick == 0,
        positives * negatives,
        jnp.where(pick == 2, positives, positives + negatives),
    )
    last = upper_part / jnp.maximum(lower_part, 1.0)
    out[:, 0, REPORT:] = jnp.broadcast_to(last, (copies, 128))


def reports_to_send(rec, copies):
    vmem = pl.BlockSpec(memory_space=pltpu.VMEM)
    sources, _, three = rec.shape
    per = three // 3
    return pl.pallas_call(
        histogram_body,
        in_specs=[vmem],
        out_specs=vmem,
        out_shape=pltpu.VMEM((copies, 1, PAYLOAD), F32),
        scratch_shapes=[
            pltpu.VMEM((sources, 8, per), F32),
            pltpu.VMEM((3, sources, per), F32),
            pltpu.VMEM((2 * HIGH + 8 * OWN, LOW), F32),
        ],
        name="histogram",
    )(in_vmem(rec))


def arrange_body(rec, reports, summary):
    parts = rec.shape[1]
    for t in range(OWN):
        for r in range(4):
            at = (t * 4 + r) * LOW
            for c in range(parts):
                to = c * RANGE + t * LOW
                reports[:, r, to : to + LOW] = rec[:, c, 0, at : at + LOW]
    rows = rec[:, 0, 0, REPORT:]
    fill = jnp.zeros((128 - rows.shape[0], 128), F32)
    summary[...] = jnp.concatenate([rows, fill], 0).T[:4, : rows.shape[0]]


def arranged(rec, intervals):
    vmem = pl.BlockSpec(memory_space=pltpu.VMEM)
    parts = rec.shape[0] // intervals
    rec = rec.reshape(intervals, parts, 1, PAYLOAD)
    reports, summary = pl.pallas_call(
        arrange_body,
        in_specs=[vmem],
        out_specs=[vmem, vmem],
        out_shape=[
            jax.ShapeDtypeStruct((intervals, 4, parts * RANGE), F32),
            jax.ShapeDtypeStruct((4, intervals), F32),
        ],
        name="arrange",
    )(in_vmem(rec))
    return reports, summary.T


def on_device(
    interact,
    weight_one,
    bias_one,
    weight_two,
    bias_two,
    weight_three,
    bias_three,
    weight_four,
    bias_four,
    weight_out,
    bias_out,
    bucket_index,
    labels,
):
    intervals, per, _ = interact.shape
    size_x, size_y, size_z = [lax.axis_size(a) for a in ALL]
    examples = examples_to_send(
        interact,
        bucket_index,
        labels,
        (weight_one, weight_two, weight_three, weight_four),
        (bias_one, bias_two, bias_three, bias_four),
        weight_out,
        bias_out,
        (size_x, 2),
    ).reshape(size_x * size_y * size_z, 1, 3 * per)
    examples = lax.all_to_all(examples, ALL, 0, 0, tiled=True)
    payload = reports_to_send(examples, size_y * size_z)
    payload = lax.all_to_all(payload, ("gy", "gz"), 0, 0, tiled=True)
    return arranged(payload, intervals)


def solution(mesh):
    split = P(None, ALL)
    in_specs = (P(None, ALL, None),) + (P(),) * 10 + (split, split)
    out_specs = (P(None, None, "gx"), P())
    return jax.shard_map(
        on_device, mesh=mesh, in_specs=in_specs, out_specs=out_specs, check_vma=False
    )
```

time: 156 us -> 67 us (0.43)
  the two profiles are of different devices: /device:TPU:0 before, /device:TPU:1 now
where the time goes in v2:
time: 67 us; the launch traced here: 66.8 us
  blocking collectives  36.7 us (55%)
  Pallas kernels  28.8 us (43%)
  between operations  1.3 us (2%)
    all_to_all x1, blocking collectives, on_device(): examples = lax.all_to_all(examples, ALL, 0, 0, tiled=True)  23.5 us
    pallas_call x1, Pallas kernels, examples_to_send(): pl.pallas_call(body, in_specs=[pl.BlockSpec(memory_space=pltpu.HBM)] * co...  22 us
    all_to_all x1, blocking collectives, on_device(): payload = lax.all_to_all(payload, ('gy', 'gz'), 0, 0, tiled=True)  13.2 us
    pallas_call x1, Pallas kernels, reports_to_send(): pl.pallas_call(histogram_body, in_specs=[vmem], out_specs=vmem, out_shape...  6.01 us

profile of v2, /device:TPU:1, one launch (start us, length us, event | category | flops | bytes accessed | tf_op | source)
XLA Modules:
  0.0 66.8 jit_solution(8766913930776667316)
XLA Ops:
  1.3 22.0 %mlp.1 = f32[4,16,2,1,768]{4,3,2,1,0:T(1,128)S(1)} custom-call(bf16[16,256,512]{2,1,0:T(8,128)(2,1)} %refs_0_.1, s32[16,256]{1,0:T(8,128)} %refs_1_.1, s32[16,256]{1,0:T(8,128)} %refs_2_.1, bf16[512,1024]{1,0:T(8,128)(2,1)} %refs_3_.1, f32[1,1024]{1,0:T(1,128)} %bitcast.10, bf16[1024,1024]{1,0:T(8,128)(2,1)} %refs_5_.1, f32[1,1024]{1,0:T(1,128)} %bitcast.11, ...), custom_call_target="tpu_custom_call" | custom-call | tf_op jit(solution)/shard_map/mlp/pallas_call | solution.py:111
  23.3 23.5 %all_to_all.10.rec = f32[128,1,768]{2,1,0:T(1,128)S(1)} all-to-all(f32[128,1,768]{2,1,0:T(1,128)S(1)} %bitcast.8), channel_id=1, replica_groups=mesh['gx'=4,'gy'=4,'gz'=8] {'gx','gy','gz'}, dimensions={0} | all-to-all | bytes 786432 | tf_op jit(solution)/shard_map/all_to_all | solution.py:286
  46.8 6.0 %histogram.1 = f32[32,1,2176]{2,1,0:T(1,128)S(1)} custom-call(f32[128,1,768]{2,1,0:T(1,128)S(1)} %all_to_all.10.rec), custom_call_target="tpu_custom_call" | custom-call | tf_op jit(solution)/shard_map/histogram/pallas_call | solution.py:215
  52.8 13.2 %all_to_all.11 = f32[32,1,2176]{2,1,0:T(1,128)S(1)} all-to-all(f32[32,1,2176]{2,1,0:T(1,128)S(1)} %histogram.1), channel_id=1, replica_groups=mesh['gx'=4,'gy'=4,'gz'=8] {'gy','gz'}, dimensions={0} | all-to-all | bytes 557056 | tf_op jit(solution)/shard_map/all_to_all | solution.py:288
  66.1 0.7 %arrange.1 = (f32[16,4,1024]{2,1,0:T(4,128)}, f32[4,16]{1,0:T(4,128)}) custom-call(f32[16,2,1,2176]{3,2,1,0:T(1,128)S(1)} %bitcast.9), custom_call_target="tpu_custom_call" | custom-call | tf_op jit(solution)/shard_map/arrange/pallas_call | solution.py:246

commit v3 on v2

--- a/solution.py
+++ b/solution.py
@@ -129,39 +129,46 @@
     )
 
 
-def histogram_body(rec, out, vals, digits, acc):
-    sources = rec.shape[0]
-    per = rec.shape[2] // 3
+def histogram_body(fields, rec, out, vals, digits, acc):
+    stride = fields * 2
+    sources = rec.shape[0] // stride
+    chunks = 2 * sources
     group = 32
     block = lax.axis_index("gx") * 2 + lax.axis_index("gz") % 2
-    bucket = rec[:, 0, :per].astype(jnp.int32)
-    y = rec[:, 0, per : 2 * per]
-    z = rec[:, 0, 2 * per :]
-    p = jax.nn.sigmoid(z)
-    loss = jax.nn.softplus(z) - y * z
-    sq = (p - y) ** 2
-    sums = []
-    for v, value in enumerate((p, loss, sq)):
-        upper = value.astype(BF16).astype(F32)
-        vals[:, 2 * v, :] = upper
-        vals[:, 2 * v + 1, :] = value - upper
-        sums.append(jnp.sum(value))
-    vals[:, 6, :] = jnp.zeros_like(y)
-    vals[:, 7, :] = jnp.zeros_like(y)
-    high = lax.shift_right_logical(bucket, 7)
-    digits[0] = (high + jnp.where(y > 0.5, 0, HIGH)).astype(F32)
-    digits[1] = jnp.bitwise_and(bucket, LOW - 1).astype(F32)
-    digits[2] = (high - block * OWN).astype(F32)
-    iota_high = lax.broadcasted_iota(jnp.int32, (2 * HIGH, per), 0).astype(F32).astype(BF16)
-    iota_low = lax.broadcasted_iota(jnp.int32, (LOW, per), 0).astype(F32).astype(BF16)
+    sums = [0.0] * 3
+    for half in range(2):
+        bucket, y, z = [
+            rec[pl.ds(2 * k + half, sources, stride=stride), :] for k in range(fields)
+        ]
+        bucket = bucket.astype(jnp.int32)
+        p = jax.nn.sigmoid(z)
+        loss = jax.nn.softplus(z) - y * z
+        sq = (p - y) ** 2
+        base = half * sources
+        for v, value in enumerate((p, loss, sq)):
+            upper = value.astype(BF16).astype(F32)
+            vals[pl.ds(8 * base + 2 * v, sources, stride=8), :] = upper
+            vals[pl.ds(8 * base + 2 * v + 1, sources, stride=8), :] = value - upper
+            sums[v] += jnp.sum(value)
+        for v in (6, 7):
+            vals[pl.ds(8 * base + v, sources, stride=8), :] = jnp.zeros_like(y)
+        high = lax.shift_right_logical(bucket, 7)
+        part = pl.ds(base, sources)
+        digits[0, part] = (high + jnp.where(y > 0.5, 0, HIGH)).astype(F32)
+        digits[1, part] = jnp.bitwise_and(bucket, LOW - 1).astype(F32)
+        digits[2, part] = (high - block * OWN).astype(F32)
+    lanes = rec.shape[1]
+    iota_high = lax.broadcasted_iota(jnp.int32, (2 * HIGH, lanes), 0).astype(F32).astype(BF16)
+    iota_low = lax.broadcasted_iota(jnp.int32, (LOW, lanes), 0).astype(F32).astype(BF16)
 
     def step(g, carry):
         left, right = [], []
         for k in range(group):
             i = g * group + k
-            own = jnp.broadcast_to(digits[2, pl.ds(i, 1), :], (8, per))
+            own = jnp.broadcast_to(digits[2, pl.ds(i, 1), :], (8, lanes))
+            value = vals[pl.ds(pl.multiple_of(8 * i, 8), 8), :]
             mine = jnp.concatenate(
-                [jnp.where(own == float(h), vals[i], 0.0) for h in range(OWN)], 0
+                [jnp.where(own == float(h), value, 0.0) for h in range(OWN)], 0
             ).astype(BF16)
             counts = one_hot_rows(digits[0, pl.ds(i, 1), :], iota_high)
             left.append(jnp.concatenate([counts, mine], 0))
@@ -169,7 +176,7 @@
         return carry + nt_dot(jnp.concatenate(left, 1), jnp.concatenate(right, 1))
 
     total = jnp.zeros((2 * HIGH + 8 * OWN, LOW), F32)
-    total = lax.fori_loop(0, sources // group, step, total)
+    total = lax.fori_loop(0, chunks // group, step, total)
     acc[...] = total
     pos, neg = total[:HIGH], total[HIGH : 2 * HIGH]
     lane = lax.broadcasted_iota(jnp.int32, neg.shape, 1)
@@ -187,15 +194,17 @@
     first = block * OWN
     own_pos, own_neg = acc[pl.ds(first, OWN)], acc[pl.ds(first + HIGH, OWN)]
     inverse = 1.0 / jnp.maximum(own_pos + own_neg, 1.0)
-    copies = out.shape[0]
+    rows_each = PAYLOAD // LOW
+    copies = out.shape[0] // rows_each
     for t in range(OWN):
         scale = inverse[t : t + 1]
         for r in range(4):
             at = 2 * HIGH + 8 * t + 2 * (r - 1)
             sum_row = total[at : at + 1] + total[at + 1 : at + 2] if r else own_pos[t : t + 1]
-            to = (t * 4 + r) * LOW
-            out[:, 0, to : to + LOW] = jnp.broadcast_to(sum_row * scale, (copies, LOW))
-    pick = lax.broadcasted_iota(jnp.int32, (1, 128), 1)
+            out[pl.ds(t * 4 + r, copies, stride=rows_each), :] = jnp.broadcast_to(
+                sum_row * scale, (copies, LOW)
+            )
+    pick = lax.broadcasted_iota(jnp.int32, (1, LOW), 1)
     upper_part = jnp.where(
         pick == 0, pairs, jnp.where(pick == 1, sums[1], jnp.where(pick == 2, sums[0], sums[2]))
     )
@@ -205,46 +214,49 @@
         jnp.where(pick == 2, positives, positives + negatives),
     )
     last = upper_part / jnp.maximum(lower_part, 1.0)
-    out[:, 0, REPORT:] = jnp.broadcast_to(last, (copies, 128))
+    out[pl.ds(rows_each - 1, copies, stride=rows_each), :] = jnp.broadcast_to(last, (copies, LOW))
 
 
 def reports_to_send(rec, copies):
     vmem = pl.BlockSpec(memory_space=pltpu.VMEM)
-    sources, _, three = rec.shape
-    per = three // 3
-    return pl.pallas_call(
-        histogram_body,
+    fields = 3
+    rec = rec.reshape(-1, LOW)
+    chunks = rec.shape[0] // fields
+    sent = pl.pallas_call(
+        lambda *refs: histogram_body(fields, *refs),
         in_specs=[vmem],
         out_specs=vmem,
-        out_shape=pltpu.VMEM((copies, 1, PAYLOAD), F32),
+        out_shape=pltpu.VMEM((copies * PAYLOAD // LOW, LOW), F32),
         scratch_shapes=[
-            pltpu.VMEM((sources, 8, per), F32),
-            pltpu.VMEM((3, sources, per), F32),
+            pltpu.VMEM((8 * chunks, LOW), F32),
+            pltpu.VMEM((3, chunks, LOW), F32),
             pltpu.VMEM((2 * HIGH + 8 * OWN, LOW), F32),
         ],
         name="histogram",
     )(in_vmem(rec))
-
-
-def arrange_body(rec, reports, summary):
-    parts = rec.shape[1]
+    return sent.reshape(copies, 1, PAYLOAD)
+
+
+def arrange_body(parts, rec, reports, summary):
+    intervals = reports.shape[0]
+    rows_each = PAYLOAD // LOW
+    stride = parts * rows_each
     for t in range(OWN):
         for r in range(4):
-            at = (t * 4 + r) * LOW
             for c in range(parts):
                 to = c * RANGE + t * LOW
-                reports[:, r, to : to + LOW] = rec[:, c, 0, at : at + LOW]
-    rows = rec[:, 0, 0, REPORT:]
-    fill = jnp.zeros((128 - rows.shape[0], 128), F32)
-    summary[...] = jnp.concatenate([rows, fill], 0).T[:4, : rows.shape[0]]
+                at = c * rows_each + t * 4 + r
+                reports[:, r, to : to + LOW] = rec[pl.ds(at, intervals, stride=stride), :]
+    rows = rec[pl.ds(rows_each - 1, intervals, stride=stride), :]
+    fill = jnp.zeros((LOW - intervals, LOW), F32)
+    summary[...] = jnp.concatenate([rows, fill], 0).T[:4, :intervals]
 
 
 def arranged(rec, intervals):
     vmem = pl.BlockSpec(memory_space=pltpu.VMEM)
     parts = rec.shape[0] // intervals
-    rec = rec.reshape(intervals, parts, 1, PAYLOAD)
     reports, summary = pl.pallas_call(
-        arrange_body,
+        lambda *refs: arrange_body(parts, *refs),
         in_specs=[vmem],
         out_specs=[vmem, vmem],
         out_shape=[
@@ -252,7 +264,7 @@
             jax.ShapeDtypeStruct((4, intervals), F32),
         ],
         name="arrange",
-    )(in_vmem(rec))
+    )(in_vmem(rec.reshape(-1, LOW)))
     return reports, summary.T
 
 

time: 67 us -> 66 us (0.985)
  Pallas kernels: 28.8 us -> 27.8 us
    pallas_call x2, Pallas kernels: 6.75 us -> 5.79 us  [the longest x1 4.88 us: reports_to_send(): pl.pallas_call(lambda *refs: histogram_body(fields, *refs), in_specs=[vme...]
where the time goes in v3:
time: 66 us; the launch traced here: 65.8 us
  blocking collectives  36.7 us (56%)
  Pallas kernels  27.8 us (42%)
  between operations  1.3 us (2%)
    all_to_all x1, blocking collectives, on_device(): examples = lax.all_to_all(examples, ALL, 0, 0, tiled=True)  23.5 us
    pallas_call x1, Pallas kernels, examples_to_send(): pl.pallas_call(body, in_specs=[pl.BlockSpec(memory_space=pltpu.HBM)] * co...  22 us
    all_to_all x1, blocking collectives, on_device(): payload = lax.all_to_all(payload, ('gy', 'gz'), 0, 0, tiled=True)  13.2 us
    pallas_call x1, Pallas kernels, reports_to_send(): pl.pallas_call(lambda *refs: histogram_body(fields, *refs), in_specs=[vme...  4.88 us

profile of v3, /device:TPU:1, one launch (start us, length us, event | category | flops | bytes accessed | tf_op | source)
XLA Modules:
  0.0 65.8 jit_solution(11922570509778452755)
XLA Ops:
  1.3 22.0 %mlp.1 = f32[4,16,2,1,768]{4,3,2,1,0:T(1,128)S(1)} custom-call(bf16[16,256,512]{2,1,0:T(8,128)(2,1)} %refs_0_.1, s32[16,256]{1,0:T(8,128)} %refs_1_.1, s32[16,256]{1,0:T(8,128)} %refs_2_.1, bf16[512,1024]{1,0:T(8,128)(2,1)} %refs_3_.1, f32[1,1024]{1,0:T(1,128)} %bitcast.14, bf16[1024,1024]{1,0:T(8,128)(2,1)} %refs_5_.1, f32[1,1024]{1,0:T(1,128)} %bitcast.15, ...), custom_call_target="tpu_custom_call" | custom-call | tf_op jit(solution)/shard_map/mlp/pallas_call | solution.py:111
  23.3 23.5 %all_to_all.10 = f32[128,1,768]{2,1,0:T(1,128)S(1)} all-to-all(f32[128,1,768]{2,1,0:T(1,128)S(1)} %bitcast.10), channel_id=1, replica_groups=mesh['gx'=4,'gy'=4,'gz'=8] {'gx','gy','gz'}, dimensions={0} | all-to-all | bytes 786432 | tf_op jit(solution)/shard_map/all_to_all | solution.py:298
  46.8 4.9 %histogram.1 = f32[544,128]{1,0:T(8,128)S(1)} custom-call(f32[768,128]{1,0:T(8,128)S(1)} %bitcast.11), custom_call_target="tpu_custom_call" | custom-call | tf_op jit(solution)/shard_map/histogram/pallas_call | solution.py:225
  51.7 13.2 %all_to_all.11 = f32[32,1,2176]{2,1,0:T(1,128)S(1)} all-to-all(f32[32,1,2176]{2,1,0:T(1,128)S(1)} %bitcast.13), channel_id=1, replica_groups=mesh['gx'=4,'gy'=4,'gz'=8] {'gy','gz'}, dimensions={0} | all-to-all | bytes 557056 | tf_op jit(solution)/shard_map/all_to_all | solution.py:300
  64.9 0.9 %arrange.1 = (f32[16,4,1024]{2,1,0:T(4,128)}, f32[4,16]{1,0:T(4,128)}) custom-call(f32[544,128]{1,0:T(8,128)S(1)} %bitcast.12), custom_call_target="tpu_custom_call" | custom-call | tf_op jit(solution)/shard_map/arrange/pallas_call | solution.py:258

commit v4 on v3

--- a/solution.py
+++ b/solution.py
@@ -14,6 +14,7 @@
 PAYLOAD = REPORT + 128
 BF16 = jnp.bfloat16
 F32 = jnp.float32
+POSITIVE = 4096.0
 
 
 def in_vmem(value):
@@ -24,7 +25,7 @@
     return lax.dot_general(a, b, (((1,), (1,)), ((), ())), preferred_element_type=F32)
 
 
-def mlp_body(steps, chains, sources, bo, out, held, sem):
+def mlp_body(steps, chains, sources, bo, out, held, last, sem):
     x, buckets, labels = held[:3]
     intervals, per, width = x.shape
     each = intervals // steps
@@ -40,9 +41,25 @@
     for copy in feeds[:1] + weights + [last_weight] + tags + feeds[1:]:
         copy.start()
 
+    def emit(k):
+        column = held[-1][...].astype(F32)
+        for i in range(each):
+            at = k * each + i
+            pieces = [buckets[pl.ds(at, 1), :].astype(F32), labels[pl.ds(at, 1), :].astype(F32)]
+            for q in range(0, per, 128):
+                h = last[pl.ds(i * per + q, 128), :].astype(F32) * column
+                h = sum(h[:, j : j + 128] for j in range(0, h.shape[1], 128))
+                pieces.append(jnp.sum(h.T, axis=0, keepdims=True) + bo[0])
+            row = jnp.concatenate(pieces, axis=1)
+            for a in range(out.shape[0]):
+                for c in range(out.shape[2]):
+                    out[a, at, c] = row
+
     def run(k, waiting):
         if waiting:
             feeds[0].wait()
+        else:
+            emit(k - 1)
         flat = x[pl.ds(k * each, each)].reshape(each * per, width)
         size = each * per // chains
         hidden = [flat[c * size : (c + 1) * size] for c in range(chains)]
@@ -57,27 +74,11 @@
                 )
                 for h in hidden
             ]
-        if waiting:
-            for copy in [last_weight] + tags:
-                copy.wait()
-        column = jnp.broadcast_to(held[-1][...], (16, held[-1].shape[1]))
-        logits = nt_dot(column, jnp.concatenate(hidden, axis=0)) + bo[0]
-        for i in range(each):
-            at = k * each + i
-            row = jnp.concatenate(
-                [
-                    buckets[pl.ds(at, 1), :].astype(F32),
-                    labels[pl.ds(at, 1), :].astype(F32),
-                    logits[0:1, i * per : (i + 1) * per],
-                ],
-                axis=1,
-            )
-            for a in range(out.shape[0]):
-                for c in range(out.shape[2]):
-                    out[a, at, c] = row
+        for c in range(chains):
+            last[pl.ds(c * size, size), :] = hidden[c]
 
     run(0, True)
-    for copy in feeds[1:]:
+    for copy in [last_weight] + tags + feeds[1:]:
         copy.wait()
 
     def step(k, carry):
@@ -85,6 +86,7 @@
         return carry
 
     lax.fori_loop(1, steps, step, 0)
+    emit(steps - 1)
 
 
 def examples_to_send(x, buckets, labels, weights, biases, wo, bo, copies):
@@ -104,7 +106,8 @@
             refs[:count],
             refs[count],
             refs[count + 1],
-            refs[count + 2 : -1],
+            refs[count + 2 : -2],
+            refs[-2],
             refs[-1],
         )
 
@@ -115,7 +118,10 @@
         out_specs=pl.BlockSpec(memory_space=pltpu.VMEM),
         out_shape=pltpu.VMEM((before, intervals, after, 1, 3 * per), F32),
         scratch_shapes=[pltpu.VMEM(a.shape, a.dtype) for a in ops]
-        + [pltpu.SemaphoreType.DMA((steps + count - 1,))],
+        + [
+            pltpu.VMEM((intervals // steps * per, wo.shape[0]), BF16),
+            pltpu.SemaphoreType.DMA((steps + count - 1,)),
+        ],
         compiler_params=pltpu.CompilerParams(vmem_limit_bytes=40 * 2**20),
         name="mlp",
     )(*[pltpu.with_memory_space_constraint(a, pltpu.HBM) for a in ops], bo)
@@ -133,7 +139,7 @@
     stride = fields * 2
     sources = rec.shape[0] // stride
     chunks = 2 * sources
-    group = 32
+    group = 16
     block = lax.axis_index("gx") * 2 + lax.axis_index("gz") % 2
     sums = [0.0] * 3
     for half in range(2):
@@ -154,31 +160,48 @@
             vals[pl.ds(8 * base + v, sources, stride=8), :] = jnp.zeros_like(y)
         high = lax.shift_right_logical(bucket, 7)
         part = pl.ds(base, sources)
-        digits[0, part] = (high + jnp.where(y > 0.5, 0, HIGH)).astype(F32)
+        digits[0, part] = high.astype(F32)
         digits[1, part] = jnp.bitwise_and(bucket, LOW - 1).astype(F32)
-        digits[2, part] = (high - block * OWN).astype(F32)
+        digits[2, part] = jnp.where(y > 0.5, POSITIVE, 1.0)
     lanes = rec.shape[1]
-    iota_high = lax.broadcasted_iota(jnp.int32, (2 * HIGH, lanes), 0).astype(F32).astype(BF16)
+    zero = jnp.zeros((), BF16)
+    iota_high = lax.broadcasted_iota(jnp.int32, (HIGH, lanes), 0).astype(F32).astype(BF16)
     iota_low = lax.broadcasted_iota(jnp.int32, (LOW, lanes), 0).astype(F32).astype(BF16)
-
-    def step(g, carry):
-        left, right = [], []
-        for k in range(group):
-            i = g * group + k
-            own = jnp.broadcast_to(digits[2, pl.ds(i, 1), :], (8, lanes))
-            value = vals[pl.ds(pl.multiple_of(8 * i, 8), 8), :]
-            mine = jnp.concatenate(
-                [jnp.where(own == float(h), value, 0.0) for h in range(OWN)], 0
-            ).astype(BF16)
-            counts = one_hot_rows(digits[0, pl.ds(i, 1), :], iota_high)
-            left.append(jnp.concatenate([counts, mine], 0))
-            right.append(one_hot_rows(digits[1, pl.ds(i, 1), :], iota_low))
-        return carry + nt_dot(jnp.concatenate(left, 1), jnp.concatenate(right, 1))
-
-    total = jnp.zeros((2 * HIGH + 8 * OWN, LOW), F32)
-    total = lax.fori_loop(0, chunks // group, step, total)
-    acc[...] = total
-    pos, neg = total[:HIGH], total[HIGH : 2 * HIGH]
+    pair = lax.broadcasted_iota(jnp.int32, (16, lanes), 0) // 8
+    own_pairs = [(block * OWN + h + pair).astype(F32).astype(BF16) for h in range(0, OWN, 2)]
+
+    def packed_row(k, i):
+        return jnp.broadcast_to(digits[k, pl.ds(i, 1), :], (16, lanes)).astype(BF16)
+
+    def hot(iota, digit, value):
+        return [
+            jnp.where(iota[k : k + 16] == digit, value, zero) for k in range(0, iota.shape[0], 16)
+        ]
+
+    def operands(i):
+        digit, weight = packed_row(0, i), packed_row(2, i)
+        value = vals[pl.ds(8 * i, 8), :]
+        value = jnp.concatenate([value, value], 0).astype(BF16)
+        left = hot(iota_high, digit, weight) + [jnp.where(m == digit, value, zero) for m in own_pairs]
+        right = hot(iota_low, packed_row(1, i), jnp.ones((), BF16))
+        return jnp.concatenate(left, 0), jnp.concatenate(right, 0)
+
+    pos = neg = total = jnp.zeros((LOW, HIGH + 8 * OWN), F32)
+    for g in range(chunks // group):
+        ops = [operands(g * group + k) for k in range(group)]
+        left = jnp.concatenate([o[0] for o in ops], 1)
+        right = jnp.concatenate([o[1] for o in ops], 1)
+        found = nt_dot(right, left)
+        some = jnp.floor(found * (1.0 / POSITIVE))
+        pos = pos + some
+        neg = neg + (found - some * POSITIVE)
+        total = total + found
+    fill = jnp.zeros((LOW, 128 - 2 * HIGH - 8 * OWN), F32)
+    wide = jnp.concatenate([pos[:, :HIGH], neg[:, :HIGH], total[:, HIGH:], fill], 1).T
+    pos, neg = wide[:HIGH], wide[HIGH : 2 * HIGH]
+    total = wide[2 * HIGH : 2 * HIGH + 8 * OWN]
+    acc[:HIGH] = pos
+    acc[HIGH:] = neg
     lane = lax.broadcasted_iota(jnp.int32, neg.shape, 1)
     sub = lax.broadcasted_iota(jnp.int32, neg.shape, 0)
     run = neg
@@ -199,7 +222,7 @@
     for t in range(OWN):
         scale = inverse[t : t + 1]
         for r in range(4):
-            at = 2 * HIGH + 8 * t + 2 * (r - 1)
+            at = 8 * t + 2 * (r - 1)
             sum_row = total[at : at + 1] + total[at + 1 : at + 2] if r else own_pos[t : t + 1]
             out[pl.ds(t * 4 + r, copies, stride=rows_each), :] = jnp.broadcast_to(
                 sum_row * scale, (copies, LOW)
@@ -230,33 +253,32 @@
         scratch_shapes=[
             pltpu.VMEM((8 * chunks, LOW), F32),
             pltpu.VMEM((3, chunks, LOW), F32),
-            pltpu.VMEM((2 * HIGH + 8 * OWN, LOW), F32),
+            pltpu.VMEM((2 * HIGH, LOW), F32),
         ],
         name="histogram",
     )(in_vmem(rec))
     return sent.reshape(copies, 1, PAYLOAD)
 
 
-def arrange_body(parts, rec, reports, summary):
-    intervals = reports.shape[0]
-    rows_each = PAYLOAD // LOW
-    stride = parts * rows_each
+def arrange_body(rec, reports, summary):
+    intervals, parts = rec.shape[:2]
     for t in range(OWN):
         for r in range(4):
+            at = (t * 4 + r) * LOW
             for c in range(parts):
                 to = c * RANGE + t * LOW
-                at = c * rows_each + t * 4 + r
-                reports[:, r, to : to + LOW] = rec[pl.ds(at, intervals, stride=stride), :]
-    rows = rec[pl.ds(rows_each - 1, intervals, stride=stride), :]
-    fill = jnp.zeros((LOW - intervals, LOW), F32)
+                reports[:, r, to : to + LOW] = rec[:, c, 0, at : at + LOW]
+    rows = rec[:, 0, 0, REPORT:]
+    fill = jnp.zeros((128 - intervals, 128), F32)
     summary[...] = jnp.concatenate([rows, fill], 0).T[:4, :intervals]
 
 
 def arranged(rec, intervals):
     vmem = pl.BlockSpec(memory_space=pltpu.VMEM)
     parts = rec.shape[0] // intervals
+    rec = rec.reshape(intervals, parts, 1, PAYLOAD)
     reports, summary = pl.pallas_call(
-        lambda *refs: arrange_body(parts, *refs),
+        arrange_body,
         in_specs=[vmem],
         out_specs=[vmem, vmem],
         out_shape=[
@@ -264,7 +286,7 @@
             jax.ShapeDtypeStruct((4, intervals), F32),
         ],
         name="arrange",
-    )(in_vmem(rec.reshape(-1, LOW)))
+    )(in_vmem(rec))
     return reports, summary.T
 
 

time: 66 us -> 63.7 us (0.965)
  Pallas kernels: 27.8 us -> 25.5 us
    pallas_call x1, Pallas kernels: 4.88 us -> 3.16 us  [reports_to_send(): pl.pallas_call(lambda *refs: histogram_body(fields, *refs), in_specs=[vme...]
where the time goes in v4:
time: 63.7 us; the launch traced here: 63.5 us
  blocking collectives  36.7 us (58%)
  Pallas kernels  25.5 us (40%)
  between operations  1.3 us (2%)
    all_to_all x1, blocking collectives, on_device(): examples = lax.all_to_all(examples, ALL, 0, 0, tiled=True)  23.5 us
    pallas_call x1, Pallas kernels, examples_to_send(): pl.pallas_call(body, in_specs=[pl.BlockSpec(memory_space=pltpu.HBM)] * co...  21.6 us
    all_to_all x1, blocking collectives, on_device(): payload = lax.all_to_all(payload, ('gy', 'gz'), 0, 0, tiled=True)  13.2 us
    pallas_call x1, Pallas kernels, reports_to_send(): pl.pallas_call(lambda *refs: histogram_body(fields, *refs), in_specs=[vme...  3.16 us

profile of v4, /device:TPU:1, one launch (start us, length us, event | category | flops | bytes accessed | tf_op | source)
XLA Modules:
  0.0 63.5 jit_solution(1159329616908791411)
XLA Ops:
  1.3 21.6 %mlp.1 = f32[4,16,2,1,768]{4,3,2,1,0:T(1,128)S(1)} custom-call(bf16[16,256,512]{2,1,0:T(8,128)(2,1)} %refs_0_.1, s32[16,256]{1,0:T(8,128)} %refs_1_.1, s32[16,256]{1,0:T(8,128)} %refs_2_.1, bf16[512,1024]{1,0:T(8,128)(2,1)} %refs_3_.1, f32[1,1024]{1,0:T(1,128)} %bitcast.14, bf16[1024,1024]{1,0:T(8,128)(2,1)} %refs_5_.1, f32[1,1024]{1,0:T(1,128)} %bitcast.15, ...), custom_call_target="tpu_custom_call" | custom-call | tf_op jit(solution)/shard_map/mlp/pallas_call | solution.py:114
  22.9 23.5 %all_to_all.10 = f32[128,1,768]{2,1,0:T(1,128)S(1)} all-to-all(f32[128,1,768]{2,1,0:T(1,128)S(1)} %bitcast.10), channel_id=1, replica_groups=mesh['gx'=4,'gy'=4,'gz'=8] {'gx','gy','gz'}, dimensions={0} | all-to-all | bytes 786432 | tf_op jit(solution)/shard_map/all_to_all | solution.py:320
  46.4 3.2 %histogram.1 = f32[544,128]{1,0:T(8,128)S(1)} custom-call(f32[768,128]{1,0:T(8,128)S(1)} %bitcast.11), custom_call_target="tpu_custom_call" | custom-call | tf_op jit(solution)/shard_map/histogram/pallas_call | solution.py:248
  49.6 13.2 %all_to_all.11 = f32[32,1,2176]{2,1,0:T(1,128)S(1)} all-to-all(f32[32,1,2176]{2,1,0:T(1,128)S(1)} %bitcast.13), channel_id=1, replica_groups=mesh['gx'=4,'gy'=4,'gz'=8] {'gy','gz'}, dimensions={0} | all-to-all | bytes 557056 | tf_op jit(solution)/shard_map/all_to_all | solution.py:322
  62.8 0.7 %arrange.1 = (f32[16,4,1024]{2,1,0:T(4,128)}, f32[4,16]{1,0:T(4,128)}) custom-call(f32[16,2,1,2176]{3,2,1,0:T(1,128)S(1)} %bitcast.12), custom_call_target="tpu_custom_call" | custom-call | tf_op jit(solution)/shard_map/arrange/pallas_call | solution.py:280

commit v5 on v4

--- a/solution.py
+++ b/solution.py
@@ -3,13 +3,14 @@
 from jax import lax
 from jax.experimental import pallas as pl
 from jax.experimental.pallas import tpu as pltpu
+from jax.sharding import Mesh
 from jax.sharding import PartitionSpec as P
 
 RANGE = 512
 LOW = 128
 OWN = RANGE // LOW
 HIGH = 4096 // LOW
-ALL = ("gx", "gy", "gz")
+ALL = ("gx", "gy", "gm", "core")
 REPORT = 4 * RANGE
 PAYLOAD = REPORT + 128
 BF16 = jnp.bfloat16
@@ -52,8 +53,7 @@
                 pieces.append(jnp.sum(h.T, axis=0, keepdims=True) + bo[0])
             row = jnp.concatenate(pieces, axis=1)
             for a in range(out.shape[0]):
-                for c in range(out.shape[2]):
-                    out[a, at, c] = row
+                out[a, at] = row
 
     def run(k, waiting):
         if waiting:
@@ -92,7 +92,6 @@
 def examples_to_send(x, buckets, labels, weights, biases, wo, bo, copies):
     intervals, per, _ = x.shape
     steps, chains = 4, 4
-    before, after = copies
     ops = [x, buckets, labels]
     for w, b in zip(weights, biases):
         ops += [w, b.reshape(1, -1)]
@@ -116,7 +115,7 @@
         in_specs=[pl.BlockSpec(memory_space=pltpu.HBM)] * count
         + [pl.BlockSpec(memory_space=pltpu.SMEM)],
         out_specs=pl.BlockSpec(memory_space=pltpu.VMEM),
-        out_shape=pltpu.VMEM((before, intervals, after, 1, 3 * per), F32),
+        out_shape=pltpu.VMEM((copies, intervals, 1, 3 * per), F32),
         scratch_shapes=[pltpu.VMEM(a.shape, a.dtype) for a in ops]
         + [
             pltpu.VMEM((intervals // steps * per, wo.shape[0]), BF16),
@@ -135,13 +134,18 @@
     )
 
 
-def histogram_body(fields, rec, out, vals, digits, acc):
+def own_block():
+    return lax.axis_index("gx") * 2 + lax.axis_index("core")
+
+
+def cell_sums(fields, rec, vals, digits):
     stride = fields * 2
     sources = rec.shape[0] // stride
     chunks = 2 * sources
     group = 16
-    block = lax.axis_index("gx") * 2 + lax.axis_index("gz") % 2
-    sums = [0.0] * 3
+    lanes = rec.shape[1]
+    block = own_block()
+    sums = [jnp.zeros((1, lanes), F32)] * 3
     for half in range(2):
         bucket, y, z = [
             rec[pl.ds(2 * k + half, sources, stride=stride), :] for k in range(fields)
@@ -155,7 +159,7 @@
             upper = value.astype(BF16).astype(F32)
             vals[pl.ds(8 * base + 2 * v, sources, stride=8), :] = upper
             vals[pl.ds(8 * base + 2 * v + 1, sources, stride=8), :] = value - upper
-            sums[v] += jnp.sum(value)
+            sums[v] += jnp.sum(value, axis=0, keepdims=True)
         for v in (6, 7):
             vals[pl.ds(8 * base + v, sources, stride=8), :] = jnp.zeros_like(y)
         high = lax.shift_right_logical(bucket, 7)
@@ -163,7 +167,6 @@
         digits[0, part] = high.astype(F32)
         digits[1, part] = jnp.bitwise_and(bucket, LOW - 1).astype(F32)
         digits[2, part] = jnp.where(y > 0.5, POSITIVE, 1.0)
-    lanes = rec.shape[1]
     zero = jnp.zeros((), BF16)
     iota_high = lax.broadcasted_iota(jnp.int32, (HIGH, lanes), 0).astype(F32).astype(BF16)
     iota_low = lax.broadcasted_iota(jnp.int32, (LOW, lanes), 0).astype(F32).astype(BF16)
@@ -196,6 +199,21 @@
         pos = pos + some
         neg = neg + (found - some * POSITIVE)
         total = total + found
+    return (pos, neg, total), sums
+
+
+def first_body(fields, rec, cells, sums, vals, digits):
+    found, rows = cell_sums(fields, rec, vals, digits)
+    for k in range(3):
+        cells[k] = found[k]
+        sums[k : k + 1] = rows[k]
+
+
+def second_body(fields, rec, cells, sums_before, out, vals, digits, acc):
+    found, rows = cell_sums(fields, rec, vals, digits)
+    pos, neg, total = [found[k] + cells[k] for k in range(3)]
+    sums = [jnp.sum(rows[k] + sums_before[k : k + 1]) for k in range(3)]
+    block = own_block()
     fill = jnp.zeros((LOW, 128 - 2 * HIGH - 8 * OWN), F32)
     wide = jnp.concatenate([pos[:, :HIGH], neg[:, :HIGH], total[:, HIGH:], fill], 1).T
     pos, neg = wide[:HIGH], wide[HIGH : 2 * HIGH]
@@ -240,23 +258,28 @@
     out[pl.ds(rows_each - 1, copies, stride=rows_each), :] = jnp.broadcast_to(last, (copies, LOW))
 
 
-def reports_to_send(rec, copies):
+def reports_to_send(rec, other, copies):
     vmem = pl.BlockSpec(memory_space=pltpu.VMEM)
     fields = 3
-    rec = rec.reshape(-1, LOW)
+    rec, other = rec.reshape(-1, LOW), other.reshape(-1, LOW)
     chunks = rec.shape[0] // fields
+    scratch = [pltpu.VMEM((8 * chunks, LOW), F32), pltpu.VMEM((3, chunks, LOW), F32)]
+    cells, sums = pl.pallas_call(
+        lambda *refs: first_body(fields, *refs),
+        in_specs=[vmem],
+        out_specs=[vmem, vmem],
+        out_shape=[pltpu.VMEM((3, LOW, HIGH + 8 * OWN), F32), pltpu.VMEM((8, LOW), F32)],
+        scratch_shapes=scratch,
+        name="histogram_first",
+    )(in_vmem(rec))
     sent = pl.pallas_call(
-        lambda *refs: histogram_body(fields, *refs),
-        in_specs=[vmem],
+        lambda *refs: second_body(fields, *refs),
+        in_specs=[vmem] * 3,
         out_specs=vmem,
         out_shape=pltpu.VMEM((copies * PAYLOAD // LOW, LOW), F32),
-        scratch_shapes=[
-            pltpu.VMEM((8 * chunks, LOW), F32),
-            pltpu.VMEM((3, chunks, LOW), F32),
-            pltpu.VMEM((2 * HIGH, LOW), F32),
-        ],
-        name="histogram",
-    )(in_vmem(rec))
+        scratch_shapes=scratch + [pltpu.VMEM((2 * HIGH, LOW), F32)],
+        name="histogram_second",
+    )(in_vmem(other), in_vmem(cells), in_vmem(sums))
     return sent.reshape(copies, 1, PAYLOAD)
 
 
@@ -306,7 +329,7 @@
     labels,
 ):
     intervals, per, _ = interact.shape
-    size_x, size_y, size_z = [lax.axis_size(a) for a in ALL]
+    size_x, size_y, size_m, size_c = [lax.axis_size(a) for a in ALL]
     examples = examples_to_send(
         interact,
         bucket_index,
@@ -315,15 +338,18 @@
         (bias_one, bias_two, bias_three, bias_four),
         weight_out,
         bias_out,
-        (size_x, 2),
-    ).reshape(size_x * size_y * size_z, 1, 3 * per)
-    examples = lax.all_to_all(examples, ALL, 0, 0, tiled=True)
-    payload = reports_to_send(examples, size_y * size_z)
-    payload = lax.all_to_all(payload, ("gy", "gz"), 0, 0, tiled=True)
+        size_x,
+    ).reshape(size_x * size_y * size_m, 1, 3 * per)
+    examples = lax.all_to_all(examples, ALL[:3], 0, 0, tiled=True)
+    others = lax.ppermute(examples, "core", [(0, 1), (1, 0)])
+    payload = reports_to_send(examples, others, size_y * size_m * size_c)
+    payload = lax.all_to_all(payload, ALL[1:], 0, 0, tiled=True)
     return arranged(payload, intervals)
 
 
 def solution(mesh):
+    x, y, z = [mesh.shape[a] for a in ("gx", "gy", "gz")]
+    mesh = Mesh(mesh.devices.reshape(x, y, z // 2, 2), ALL)
     split = P(None, ALL)
     in_specs = (P(None, ALL, None),) + (P(),) * 10 + (split, split)
     out_specs = (P(None, None, "gx"), P())

time: 63.7 us -> 62.4 us (0.980)
  blocking collectives: 36.7 us -> 33.1 us
  starting transfers between devices: 0 us -> 2.1 us
    all_to_all x2, blocking collectives: 36.7 us -> 33.1 us  [the longest x1 20.9 us: on_device(): examples = lax.all_to_all(examples, ALL[:3], 0, 0, tiled=True)]
    ppermute x0 -> x1, starting transfers between devices: none -> 2.1 us  [on_device(): others = lax.ppermute(examples, 'core', [(0, 1), (1, 0)])]
    pallas_call x1 -> x2, Pallas kernels: 3.16 us -> 3.34 us  [the longest x1 2.04 us: reports_to_send(): pl.pallas_call(lambda *refs: second_body(fields, *refs), in_specs=[vmem]...]
  transfers between devices with their start and end apart: 0 -> 1, of which waited for: 0 -> 0; matrix products, arithmetic and copies ran while one was open for 0% -> 0% of each run, Pallas kernels for 0% -> 2%
where the time goes in v5:
time: 62.4 us; the launch traced here: 62.2 us
  blocking collectives  33.1 us (53%)
  Pallas kernels  25.7 us (41%)
  starting transfers between devices  2.1 us (3%)
  between operations  1.31 us (2%)
    pallas_call x1, Pallas kernels, examples_to_send(): pl.pallas_call(body, in_specs=[pl.BlockSpec(memory_space=pltpu.HBM)] * co...  21.6 us
    all_to_all x1, blocking collectives, on_device(): examples = lax.all_to_all(examples, ALL[:3], 0, 0, tiled=True)  20.9 us
    all_to_all x1, blocking collectives, on_device(): payload = lax.all_to_all(payload, ALL[1:], 0, 0, tiled=True)  12.2 us
    ppermute x1, starting transfers between devices, on_device(): others = lax.ppermute(examples, 'core', [(0, 1), (1, 0)])  2.1 us
    pallas_call x1, Pallas kernels, reports_to_send(): pl.pallas_call(lambda *refs: second_body(fields, *refs), in_specs=[vmem]...  2.04 us
    pallas_call x1, Pallas kernels, reports_to_send(): pl.pallas_call(lambda *refs: first_body(fields, *refs), in_specs=[vmem],...  1.3 us
  transfers between devices with their start and end apart: 1, of which 0 were waited for; matrix products, arithmetic and copies ran while one was open for 0% of the time, Pallas kernels for 2%

profile of v5, /device:TPU:1, one launch (start us, length us, event | category | flops | bytes accessed | tf_op | source)
XLA Modules:
  0.0 62.2 jit_solution(13356662989502973215)
XLA Ops:
  1.3 21.6 %mlp.1 = f32[4,16,1,768]{3,2,1,0:T(1,128)S(1)} custom-call(bf16[16,256,512]{2,1,0:T(8,128)(2,1)} %refs_0_.1, s32[16,256]{1,0:T(8,128)} %refs_1_.1, s32[16,256]{1,0:T(8,128)} %refs_2_.1, bf16[512,1024]{1,0:T(8,128)(2,1)} %refs_3_.1, f32[1,1024]{1,0:T(1,128)} %bitcast.16, bf16[1024,1024]{1,0:T(8,128)(2,1)} %refs_5_.1, f32[1,1024]{1,0:T(1,128)} %bitcast.17, ...), custom_call_target="tpu_custom_call" | custom-call | tf_op jit(solution)/shard_map/mlp/pallas_call | solution.py:113
  22.9 20.9 %all_to_all.10 = f32[64,1,768]{2,1,0:T(1,128)S(1)} all-to-all(f32[64,1,768]{2,1,0:T(1,128)S(1)} %bitcast.14), channel_id=1, replica_groups=mesh['gx'=4,'gy'=4,'gm'=4,'core'=2] {'gx','gy','gm'}, dimensions={0} | all-to-all | bytes 393216 | tf_op jit(solution)/shard_map/all_to_all | solution.py:343
  43.8 2.1 %collective-permute-start = (f32[64,1,768]{2,1,0:T(1,128)S(1)}, f32[64,1,768]{2,1,0:T(1,128)S(1)}, u32[]{:S(2)}, u32[]{:S(2)}) collective-permute-start(f32[64,1,768]{2,1,0:T(1,128)S(1)} %all_to_all.10), channel_id=1, source_target_pairs={{0,1},{1,0},{2,3},{3,2},{4,5},{5,4},{6,7},{7,6},{8,9},{9,8},{10,11... | collective-permute-start | bytes 589832 | tf_op jit(solution)/shard_map/ppermute | solution.py:344
  45.9 1.3 %histogram_first.1 = (f32[3,128,64]{2,1,0:T(8,128)S(1)}, f32[8,128]{1,0:T(8,128)S(1)}) custom-call(f32[384,128]{1,0:T(8,128)S(1)} %bitcast.13), custom_call_target="tpu_custom_call" | custom-call | tf_op jit(solution)/shard_map/histogram_first/pallas_call | solution.py:267
  47.2 0.0 collective-permute-done
  47.2 2.0 %histogram_second.1 = f32[544,128]{1,0:T(8,128)S(1)} custom-call(f32[384,128]{1,0:T(8,128)S(1)} %bitcast.15, f32[3,128,64]{2,1,0:T(8,128)S(1)} %get-tuple-element.6.refs_1_, f32[8,128]{1,0:T(8,128)S(1)} %get-tuple-element.7.refs_2_), custom_call_target="tpu_custom_call" | custom-call | tf_op jit(solution)/shard_map/histogram_second/pallas_call | solution.py:275
  49.2 12.2 %all_to_all.11 = f32[32,1,2176]{2,1,0:T(1,128)S(1)} all-to-all(f32[32,1,2176]{2,1,0:T(1,128)S(1)} %bitcast.11), channel_id=1, replica_groups=mesh['gx'=4,'gy'=4,'gm'=4,'core'=2] {'gy','gm','core'}, dimensions={0} | all-to-all | bytes 557056 | tf_op jit(solution)/shard_map/all_to_all | solution.py:346
  61.5 0.7 %arrange.1 = (f32[16,4,1024]{2,1,0:T(4,128)}, f32[4,16]{1,0:T(4,128)}) custom-call(f32[16,2,1,2176]{3,2,1,0:T(1,128)S(1)} %bitcast.12), custom_call_target="tpu_custom_call" | custom-call | tf_op jit(solution)/shard_map/arrange/pallas_call | solution.py:303
Async XLA Ops:
  43.8 3.4 %collective-permute-start = (f32[64,1,768]{2,1,0:T(1,128)S(1)}, f32[64,1,768]{2,1,0:T(1,128)S(1)}, u32[]{:S(2)}, u32[]{:S(2)}) collective-permute-start(f32[64,1,768]{2,1,0:T(1,128)S(1)} %all_to_all.10), channel_id=1, source_target_pairs={{0,1},{1,0},{2,3},{3,2},{4,5},{5,4},{6,7},{7,6},{8,9},{9,8},{10,11... | collective-permute-start | bytes 589832 | tf_op jit(solution)/shard_map/ppermute | solution.py:344
